TPU v7x, 32 devices: a whole 2x2x4 slice. The times are simulated.
32 devices in a mesh: dom: 8 (over y, x, core), grp: 4 (over z).
Axes of the slice: x: 2, y: 2, z: 4, core: 2. Of those that a mesh axis runs over, the one named last changes fastest.
Arguments:
- features: bfloat16 [65536, 256], P(('dom', 'grp')), may hold values from -6 to 6
- edge_src: int32 [524288], P(('dom', 'grp')), may hold values from 0 to 2303, as said below
- edge_dst: int32 [524288], P(('dom', 'grp')), may hold values from 0 to 2047, as said below
- edge_count: int32 [32], P(('dom', 'grp')), may hold values from 4096 to 16384, as said below
- halo_index: int32 [32, 32, 8], P(('dom', 'grp')), may hold values from 0 to 2047
- request_rows: int32 [32, 32, 16], P(('dom', 'grp')), may hold values from 0 to 2047, as said below
- pair_ends: int32 [65536, 2], P(('dom', 'grp')), may hold values from 0 to 511
- labels: int32 [65536], P(('dom', 'grp')), may hold values 0 or 1
- pair_weight: float32 [65536], P(('dom', 'grp')), may hold values from 0.25 to 4
- w_self: bfloat16 [256, 256], replicated, may hold values from -0.375 to 0.375
- w_neigh: bfloat16 [256, 256], replicated, may hold values from -0.375 to 0.375
- w_hidden: bfloat16 [512, 256], replicated, may hold values from -0.25 to 0.25
- b_hidden: float32 [256], replicated, may hold values from -3 to 3
- w_out: float32 [256], replicated, may hold values from -0.375 to 0.375
Outputs:
- logits: float32 [65536], P(('dom', 'grp'))
- grad_features: float32 [65536, 256], P(('dom', 'grp'))
- grad_w_self: float32 [256, 256], replicated
- grad_w_neigh: float32 [256, 256], replicated
- grad_w_hidden: float32 [512, 256], replicated
- grad_b_hidden: float32 [256], replicated
- grad_w_out: float32 [256], replicated
Inputs may be any that keep to these rules, and one draw needn't show every extreme that they name: `edge_src`: a row of the partition's own table. `edge_dst`: a local node of the partition; slots at or past edge_count are not live and hold arbitrary values. `edge_count`: some partition has exactly 16384 live slots. `halo_index`: local rows of the sending partition; 8 to every partition, itself included. `request_rows`: local rows of the owning partition, distinct and increasing within each list of 16. `pair_ends`: rows of the shard's own received rows.
All inputs are finite; a program needn't handle non-finite values. No bound on the sum of `labels` on one device may be relied on, other than what follows from the above.
Results may differ from a plain program's by a relative error of at most 0.02.
The roundings to bfloat16 on the way count: a program that leaves them out, or rounds other values in their place, can miss the bound.
Values may be sent and summed in bfloat16 or wider, within the bound.
A program may use at most 192 MiB of HBM per device.

v0:
```python
import functools

import jax
import jax.numpy as jnp
from jax import lax
from jax.experimental import pallas as pl
from jax.experimental.pallas import tpu as pltpu
from jax.sharding import PartitionSpec as P

F32 = jnp.float32
BF16 = jnp.bfloat16
F8 = jnp.float8_e4m3fn
VMEM_LIMIT = 60 * 1024 * 1024
NN = (((1,), (0,)), ((), ()))
NT = (((1,), (1,)), ((), ()))
TN = (((0,), (0,)), ((), ()))


def dot(left, right, dims=NN):
    return lax.dot_general(left, right, dims, preferred_element_type=F32)


def column_of(row):
    return jnp.broadcast_to(row, (128, row.shape[1])).T[:, :1]


def row_of(column):
    return jnp.broadcast_to(column, (column.shape[0], 128)).T[:1, :]


def equal_mask(left, right):
    return jnp.where(left == right, 1.0, 0.0).astype(BF16)


def iota(shape, dim):
    return lax.broadcasted_iota(jnp.int32, shape, dim).astype(F32)


class Links:
    def __init__(self, peers, grp):
        self.peers, self.grp = peers, grp
        self.me = lax.axis_index("dom") * grp + lax.axis_index("grp")

    def device(self, peer):
        return {"dom": peer // self.grp, "grp": lax.rem(peer, self.grp)}

    def other(self, step):
        return lax.rem(self.me + step, self.peers)

    def each(self, body):
        def step(i, carry):
            body(self.other(i))
            return carry

        lax.fori_loop(1, self.peers, step, 0)

    def greet(self):
        barrier = pltpu.get_barrier_semaphore()
        self.each(lambda peer: pl.semaphore_signal(
            barrier, inc=1, device_id=self.device(peer), device_id_type=pl.DeviceIdType.MESH))

    def greeted(self):
        pl.semaphore_wait(pltpu.get_barrier_semaphore(), self.peers - 1)

    def copy(self, src, dst, send, recv, peer, slot):
        return pltpu.make_async_remote_copy(
            src_ref=src, dst_ref=dst, send_sem=send.at[peer], recv_sem=recv.at[slot],
            device_id=self.device(peer), device_id_type=pl.DeviceIdType.MESH)

    def start(self, moves):
        def one(peer):
            for pick, dst, send, recv in moves:
                self.copy(pick(peer), dst.at[self.me], send, recv, peer, self.me).start()

        self.each(one)

    def finish(self, moves):
        def one(peer):
            for pick, dst, send, recv in moves:
                copy = self.copy(pick(peer), dst.at[peer], send, recv, peer, peer)
                copy.wait_recv()
                copy.wait_send()

        self.each(one)


def block_of(ref):
    return lambda peer: ref.at[peer]


def whole_of(ref):
    return lambda peer: ref


def sems(peers, count):
    return [pltpu.SemaphoreType.DMA((peers,)) for _ in range(2 * count)]


def call(body, outs, args, scratch=(), collective_id=None, smem=()):
    params = dict(vmem_limit_bytes=VMEM_LIMIT)
    if collective_id is not None:
        params.update(collective_id=collective_id, has_side_effects=True)
    return pl.pallas_call(
        body,
        out_shape=tuple(jax.ShapeDtypeStruct(s, d) for s, d in outs),
        in_specs=[
            pl.BlockSpec(memory_space=pltpu.SMEM if i in smem else pltpu.VMEM)
            for i in range(len(args))
        ],
        out_specs=tuple(pl.BlockSpec(memory_space=pltpu.VMEM) for _ in outs),
        scratch_shapes=list(scratch),
        compiler_params=pltpu.CompilerParams(**params),
    )(*args)


def first_exchange(peers, grp, feat, halo_row, request, wanted, arrived, outgoing, s0, r0, s1, r1):
    links = Links(peers, grp)
    links.greet()
    halo_len, width = outgoing.shape[1:]
    nodes = feat.shape[0]
    index = column_of(halo_row[...].astype(F32))
    pick = equal_mask(index, iota((index.shape[0], nodes), 1))
    outgoing[...] = dot(pick, feat[...]).astype(BF16).reshape(outgoing.shape)
    links.greeted()
    moves = [(block_of(request), wanted, s0, r0), (block_of(outgoing), arrived, s1, r1)]
    links.start(moves)
    wanted[links.me] = request[links.me]
    arrived[links.me] = outgoing[links.me]
    links.finish(moves)


def swap_blocks(peers, grp, sent, got, s0, r0):
    links = Links(peers, grp)
    links.greet()
    links.greeted()
    moves = [(block_of(sent), got, s0, r0)]
    links.start(moves)
    got[links.me] = sent[links.me]
    links.finish(moves)


def swap_grads(peers, grp, rows, terms, small, got, got_terms, got_small, s0, r0, s1, r1, s2, r2):
    links = Links(peers, grp)
    links.greet()
    links.greeted()
    moves = [
        (block_of(rows), got, s0, r0),
        (block_of(terms), got_terms, s1, r1),
        (whole_of(small), got_small, s2, r2),
    ]
    links.start(moves)
    got[links.me] = rows[links.me]
    got_terms[links.me] = terms[links.me]
    got_small[links.me] = small[...]
    links.finish(moves)


def last_exchange(
    peers, grp, halo, terms_s, terms_n, in_hidden,
    got, all_s, all_n, all_h, in_s, in_n, own_s, own_n, own_h,
    s0, r0, s1, r1, s2, r2, s3, r3, s4, r4, s5, r5,
):
    links = Links(peers, grp)
    me = links.me
    links.greet()
    own_h[...] = jnp.sum(in_hidden[...].astype(F32), axis=0).astype(BF16)
    links.greeted()
    terms = [(block_of(terms_s), in_s, s1, r1), (block_of(terms_n), in_n, s2, r2)]
    late = [(block_of(halo), got, s0, r0), (whole_of(own_h), all_h, s5, r5)]
    links.start(terms)
    links.start(late)
    in_s[me] = terms_s[me]
    in_n[me] = terms_n[me]
    got[me] = halo[me]
    all_h[me] = own_h[...]
    links.finish(terms)
    own_s[...] = jnp.sum(in_s[...].astype(F32), axis=0).astype(BF16)
    own_n[...] = jnp.sum(in_n[...].astype(F32), axis=0).astype(BF16)
    sums = [(whole_of(own_s), all_s, s3, r3), (whole_of(own_n), all_n, s4, r4)]
    links.start(sums)
    all_s[me] = own_s[...]
    all_n[me] = own_n[...]
    links.finish(late)
    links.finish(sums)


def wanted_column(wanted, req_len):
    peers = wanted.shape[0]
    spread = jnp.broadcast_to(wanted[...].astype(F32), (peers, req_len, 128)).reshape(peers * req_len, 128)
    lane = lax.broadcasted_iota(jnp.int32, spread.shape, 1)
    row = lax.rem(lax.broadcasted_iota(jnp.int32, spread.shape, 0), req_len)
    return jnp.sum(jnp.where(lane == row, spread, 0.0), axis=1, keepdims=True)


def count_edges(req_len, chunk, block, src, dst, count, wanted, counts, total, marks, ladder):
    rows, table_rows = counts.shape
    slots = src.shape[1]
    total[...] = jnp.zeros_like(total)
    index = wanted_column(wanted, req_len)
    ladder[...] = iota(ladder.shape, 0).astype(BF16)

    @pl.loop(0, slots // chunk)
    def _(c):
        span = pl.ds(pl.multiple_of(c * chunk, chunk), chunk)
        place = lax.broadcasted_iota(jnp.int32, (1, chunk), 1) + c * chunk
        into = jnp.where(place < count[0], dst[:, span], -1).astype(F32)
        marks[...] = jnp.where(index == into, 1.0, 0.0).astype(F8)
        source = src[:, span]
        high = source // block
        low = lax.rem(source, block)

        @pl.loop(0, table_rows // block)
        def _(b):
            here = jnp.where(high == b, low, -1).astype(F32).astype(BF16)
            hit = jnp.where(ladder[...] == here, jnp.array(1, BF16), jnp.array(0, BF16)).astype(F8)
            cols = pl.ds(pl.multiple_of(b * block, block), block)
            total[:, cols] += dot(marks[...], hit, NT)

    counts[...] = total[...].astype(BF16)


def encode(req_len, block, feat, arrived, counts, wanted, w_self, w_neigh, served, feat_w, agg_w, floor):
    nodes, width = feat.shape
    rows, table_rows = counts.shape
    peers, halo_len = arrived.shape[:2]
    index = wanted_column(wanted, req_len)
    degree = jnp.sum(counts[...].astype(F32), axis=1, keepdims=True)
    floor_deg = jnp.maximum(degree, 1.0)
    sums = dot(counts[:, :nodes], feat[...])
    sums += dot(counts[:, nodes:], arrived[...].reshape(peers * halo_len, width))
    agg = (sums / floor_deg).astype(BF16)
    pick = equal_mask(index, iota((rows, nodes), 1))
    own = dot(pick, feat[...]).astype(BF16)
    emb = (dot(own, w_self[...]) + dot(agg, w_neigh[...])).astype(BF16)
    served[...] = emb.reshape(served.shape)
    feat_w[...] = own
    agg_w[...] = agg
    floor[...] = jnp.broadcast_to(floor_deg, floor.shape)


def encode_back(
    req_len, block, back, wanted, counts, feat_w, agg_w, floor, w_self, w_neigh,
    local, returned, grad_self, grad_neigh, near, far,
):
    nodes, width = local.shape
    rows, table_rows = counts.shape
    index = wanted_column(wanted, req_len)
    other = row_of(index)
    same = index == other
    earlier = lax.broadcasted_iota(jnp.int32, (rows, rows), 1) < lax.broadcasted_iota(jnp.int32, (rows, rows), 0)
    seen = jnp.sum(jnp.where(same & earlier, 1.0, 0.0), axis=1, keepdims=True)
    grad = dot(jnp.where(same, 1.0, 0.0).astype(BF16), back[...].reshape(rows, width))
    grad = jnp.where(seen > 0.0, 0.0, grad).astype(BF16)
    grad_self[...] = dot(feat_w[...], grad, TN).astype(BF16).reshape(grad_self.shape)
    grad_neigh[...] = dot(agg_w[...], grad, TN).astype(BF16).reshape(grad_neigh.shape)
    near[...] = dot(grad, w_self[...], NT).astype(BF16)
    far[...] = (dot(grad, w_neigh[...], NT) / floor[:, :1]).astype(BF16)

    @pl.loop(0, nodes // block)
    def _(b):
        cols = pl.ds(pl.multiple_of(b * block, block), block)
        spot = lax.broadcasted_iota(jnp.int32, (1, block), 1) + b * block
        pick = equal_mask(index, spot.astype(F32))
        local[cols, :] = dot(counts[:, cols], far[...], TN) + dot(pick, near[...], TN)

    halo = dot(counts[:, nodes:], far[...], TN)
    returned[...] = halo.astype(BF16).reshape(returned.shape)


def decode(
    chunk, received, ends, labels, weight, w_hidden, bias, w_out,
    logits, back, grad_hidden, small, picks, left_right, sums,
):
    peers, req_len, width = received.shape
    rows = peers * req_len
    got = received[...].reshape(rows, width)
    for place, half in ((0, w_hidden[:width, :]), (rows, w_hidden[width:, :])):
        exact = dot(got, half).T
        upper = exact.astype(BF16)
        left_right[0, :, place : place + rows] = upper
        left_right[1, :, place : place + rows] = (exact - upper.astype(F32)).astype(BF16)
    bias_col = column_of(bias[...])
    out_col = column_of(w_out[...])
    sums[...] = jnp.zeros_like(sums)
    slots = iota((rows, chunk), 0)

    def step(c, carry):
        bias_sum, out_sum = carry
        span = pl.ds(pl.multiple_of(c * chunk, chunk), chunk)
        end = ends[:, span].astype(F32)
        picks[:rows, :] = equal_mask(slots, end[:1, :])
        picks[rows:, :] = equal_mask(slots, end[1:, :])
        pre = dot(left_right[0], picks[...]) + dot(left_right[1], picks[...]) + bias_col
        hidden = jnp.maximum(pre, 0.0)
        logit = jnp.sum(hidden * out_col, axis=0, keepdims=True)
        logits[:, span] = logit
        slope = weight[:, span] * (jax.nn.sigmoid(logit) - labels[:, span].astype(F32))
        delta = jnp.where(pre > 0, slope * out_col, 0.0)
        sums[...] += dot(picks[...], delta.astype(BF16), NT)
        return (
            bias_sum + jnp.sum(delta, axis=1, keepdims=True),
            out_sum + jnp.sum(hidden * slope, axis=1, keepdims=True),
        )

    zero = jnp.zeros((width, 1), F32)
    bias_sum, out_sum = lax.fori_loop(0, ends.shape[1] // chunk, step, (zero, zero))
    small[0:1, :] = row_of(bias_sum)
    small[1:2, :] = row_of(out_sum)
    left = sums[:rows, :].astype(BF16)
    right = sums[rows:, :].astype(BF16)
    half = grad_hidden.shape[0] // 2
    shape = (half,) + grad_hidden.shape[1:]
    grad_hidden[:half] = dot(got, left, TN).astype(BF16).reshape(shape)
    grad_hidden[half:] = dot(got, right, TN).astype(BF16).reshape(shape)
    back_rows = dot(left, w_hidden[:width, :], NT) + dot(right, w_hidden[width:, :], NT)
    back[...] = back_rows.astype(BF16).reshape(back.shape)


def finish(local, halo_back, halo_row, in_s, in_n, in_h, in_small, out, g_s, g_n, g_h, g_b, g_o):
    nodes, width = local.shape
    rows = halo_row.shape[1]
    pick = equal_mask(iota((nodes, rows), 0), halo_row[...].astype(F32))
    out[...] = local[...] + dot(pick, halo_back[...].reshape(rows, width))
    g_s[...] = in_s[...].astype(F32).reshape(g_s.shape)
    g_n[...] = in_n[...].astype(F32).reshape(g_n.shape)
    g_h[...] = in_h[...].astype(F32).reshape(g_h.shape)
    small = jnp.sum(in_small[...], axis=0)
    g_b[...] = small[0:1, :]
    g_o[...] = small[1:2, :]


def per_device(
    features, edge_src, edge_dst, edge_count, halo_index, request_rows, pair_ends,
    labels, pair_weight, w_self, w_neigh, w_hidden, b_hidden, w_out,
):
    nodes, width = features.shape
    grp = lax.axis_size("grp")
    peers = lax.axis_size("dom") * grp
    halo_len = halo_index.shape[2]
    req_len = request_rows.shape[2]
    slots = edge_src.shape[0]
    pairs = labels.shape[0]
    table_rows = nodes + peers * halo_len
    rows = peers * req_len
    block = 256
    part = width // peers
    hidden_part = 2 * width // peers

    halo_row = halo_index.reshape(1, peers * halo_len)
    request = jnp.pad(request_rows[0], ((0, 0), (0, 128 - req_len))).reshape(peers, 1, 128)
    wanted, arrived = call(
        functools.partial(first_exchange, peers, grp),
        [((peers, 1, 128), jnp.int32), ((peers, halo_len, width), BF16)],
        (features, halo_row, request),
        [pltpu.VMEM((peers, halo_len, width), BF16)] + sems(peers, 2),
        collective_id=0,
    )
    edge_chunk = 2048
    (counts,) = call(
        functools.partial(count_edges, req_len, edge_chunk, block),
        [((rows, table_rows), BF16)],
        (edge_src.reshape(1, slots), edge_dst.reshape(1, slots), edge_count, wanted),
        [
            pltpu.VMEM((rows, table_rows), F32),
            pltpu.VMEM((rows, edge_chunk), F8),
            pltpu.VMEM((block, edge_chunk), BF16),
        ],
        smem=(2,),
    )
    served, feat_w, agg_w, floor = call(
        functools.partial(encode, req_len, block),
        [
            ((peers, req_len, width), BF16),
            ((rows, width), BF16),
            ((rows, width), BF16),
            ((rows, 128), F32),
        ],
        (features, arrived, counts, wanted, w_self, w_neigh),
    )
    (received,) = call(
        functools.partial(swap_blocks, peers, grp),
        [((peers, req_len, width), BF16)],
        (served,),
        sems(peers, 1),
        collective_id=1,
    )
    pair_chunk = 512
    logits, back_sent, hidden_terms, small = call(
        functools.partial(decode, pair_chunk),
        [
            ((1, pairs), F32),
            ((peers, req_len, width), BF16),
            ((peers, hidden_part, width), BF16),
            ((2, width), F32),
        ],
        (
            received, pair_ends.T, labels.reshape(1, pairs), pair_weight.reshape(1, pairs),
            w_hidden, b_hidden.reshape(1, width), w_out.reshape(1, width),
        ),
        [
            pltpu.VMEM((2 * rows, pair_chunk), BF16),
            pltpu.VMEM((2, width, 2 * rows), BF16),
            pltpu.VMEM((2 * rows, width), F32),
        ],
    )
    back, in_hidden, in_small = call(
        functools.partial(swap_grads, peers, grp),
        [
            ((peers, req_len, width), BF16),
            ((peers, hidden_part, width), BF16),
            ((peers, 2, width), F32),
        ],
        (back_sent, hidden_terms, small),
        sems(peers, 3),
        collective_id=2,
    )
    local, returned, terms_s, terms_n = call(
        functools.partial(encode_back, req_len, block),
        [
            ((nodes, width), F32),
            ((peers, halo_len, width), BF16),
            ((peers, part, width), BF16),
            ((peers, part, width), BF16),
        ],
        (back, wanted, counts, feat_w, agg_w, floor, w_self, w_neigh),
        [pltpu.VMEM((rows, width), BF16), pltpu.VMEM((rows, width), BF16)],
    )
    halo_back, all_s, all_n, all_h = call(
        functools.partial(last_exchange, peers, grp),
        [
            ((peers, halo_len, width), BF16),
            ((peers, part, width), BF16),
            ((peers, part, width), BF16),
            ((peers, hidden_part, width), BF16),
        ],
        (returned, terms_s, terms_n, in_hidden),
        [
            pltpu.VMEM((peers, part, width), BF16),
            pltpu.VMEM((peers, part, width), BF16),
            pltpu.VMEM((part, width), BF16),
            pltpu.VMEM((part, width), BF16),
            pltpu.VMEM((hidden_part, width), BF16),
        ] + sems(peers, 6),
        collective_id=3,
    )
    grad_features, g_s, g_n, g_h, g_b, g_o = call(
        finish,
        [
            ((nodes, width), F32),
            ((width, width), F32),
            ((width, width), F32),
            ((2 * width, width), F32),
            ((1, width), F32),
            ((1, width), F32),
        ],
        (local, halo_back, halo_row, all_s, all_n, all_h, in_small),
    )
    return (logits.reshape(pairs), grad_features, g_s, g_n, g_h, g_b.reshape(width), g_o.reshape(width))


def solution(mesh):
    both = ("dom", "grp")
    in_specs = (
        P(both, None), P(both), P(both), P(both), P(both, None, None), P(both, None, None),
        P(both, None), P(both), P(both), P(), P(), P(), P(), P(),
    )
    out_specs = (P(both), P(both, None), P(), P(), P(), P(), P())
    return jax.shard_map(
        per_device, mesh=mesh, in_specs=in_specs, out_specs=out_specs, check_vma=False
    )
```

profile of v0, /device:TPU:0, one launch (start us, length us, event | category | flops | bytes accessed | tf_op | source)
XLA Modules:
  0.0 146.9 jit_solution(8536047678827658916)
XLA Ops:
  1.3 0.8 copy.23
  2.0 0.7 reshape.47.halo_row
  2.7 0.8 copy.24
  3.5 0.6 pad.4
  4.1 15.0 %shard_map.189 = (s32[32,1,128]{2,1,0:T(1,128)}, bf16[32,8,256]{2,1,0:T(8,128)(2,1)}) custom-call(bf16[2048,256]{1,0:T(8,128)(2,1)} %feat.3, s32[1,256]{1,0:T(1,128)} %reshape.47.halo_row, s32[32,1,128]{2,1,0:T(1,128)} %bitcast.12), custom_call_target="tpu_custom_call" | custom-call | tf_op jit(solution)/shard_map/pallas_call | solution.py:103
  19.1 37.2 %shard_map.190.counts = bf16[512,2304]{1,0:T(8,128)(2,1)} custom-call(s32[1,16384]{1,0:T(1,128)} %bitcast.13, s32[1,16384]{1,0:T(1,128)} %bitcast.14, s32[1]{0:T(128)S(6)} %copy.25.count, s32[32,1,128]{2,1,0:T(1,128)} %get-tuple-element.35.wanted), custom_call_target="tpu_custom_call" | custom-call | tf_op jit(solution)/shard_map/pallas_call | solution.py:103
  56.3 4.6 %shard_map.191 = (bf16[32,16,256]{2,1,0:T(8,128)(2,1)}, bf16[512,256]{1,0:T(8,128)(2,1)}, bf16[512,256]{1,0:T(8,128)(2,1)}, f32[512,128]{1,0:T(8,128)}) custom-call(bf16[2048,256]{1,0:T(8,128)(2,1)} %feat.3, bf16[32,8,256]{2,1,0:T(8,128)(2,1)} %get-tuple-element.34.arrived, bf16[512,2304]{1,0:T(8,128)(2,1)} %shard_map.190.counts, ...), custom_call_target="tpu_custom_call" | custom-call | tf_op jit(solution)/shard_map/pallas_call | solution.py:103
  60.9 13.7 %shard_map.192.received = bf16[32,16,256]{2,1,0:T(8,128)(2,1)} custom-call(bf16[32,16,256]{2,1,0:T(8,128)(2,1)} %get-tuple-element.36.sent), custom_call_target="tpu_custom_call" | custom-call | tf_op jit(solution)/shard_map/pallas_call | solution.py:103
  74.6 8.3 %shard_map.193 = (f32[1,2048]{1,0:T(1,128)}, bf16[32,16,256]{2,1,0:T(8,128)(2,1)}, bf16[32,16,256]{2,1,0:T(8,128)(2,1)}, f32[2,256]{1,0:T(2,128)}) custom-call(bf16[32,16,256]{2,1,0:T(8,128)(2,1)} %shard_map.192.received, s32[2,2048]{1,0:T(2,128)} %bitcast.16, s32[1,2048]{1,0:T(1,128)} %bitcast.17, f32[1,2048]{1,0:T(1,128)} %bitcast.18, ...), custom_call_target="tpu_custom_call" | custom-call | tf_op jit(solution)/shard_map/pallas_call | solution.py:103
  82.9 22.0 %shard_map.194 = (bf16[32,16,256]{2,1,0:T(8,128)(2,1)}, bf16[32,16,256]{2,1,0:T(8,128)(2,1)}, f32[32,2,256]{2,1,0:T(2,128)}) custom-call(bf16[32,16,256]{2,1,0:T(8,128)(2,1)} %get-tuple-element.38.rows, bf16[32,16,256]{2,1,0:T(8,128)(2,1)} %get-tuple-element.39.terms, f32[2,256]{1,0:T(2,128)} %get-tuple-element.40.small), custom_call_target="tpu_custom_call" | custom-call | tf_op jit(solution)/shard_map/pallas_call | solution.py:103
  104.9 7.2 %shard_map.195 = (f32[2048,256]{1,0:T(8,128)}, bf16[32,8,256]{2,1,0:T(8,128)(2,1)}, bf16[32,8,256]{2,1,0:T(8,128)(2,1)}, bf16[32,8,256]{2,1,0:T(8,128)(2,1)}) custom-call(bf16[32,16,256]{2,1,0:T(8,128)(2,1)} %get-tuple-element.41.back, s32[32,1,128]{2,1,0:T(1,128)} %get-tuple-element.35.wanted, bf16[512,2304]{1,0:T(8,128)(2,1)} %shard_map.190.counts, ...), custom_call_target="tpu_custom_call" | custom-call | tf_op jit(solution)/shard_map/pallas_call | solution.py:103
  112.1 30.8 %shard_map.196 = (bf16[32,8,256]{2,1,0:T(8,128)(2,1)}, bf16[32,8,256]{2,1,0:T(8,128)(2,1)}, bf16[32,8,256]{2,1,0:T(8,128)(2,1)}, bf16[32,16,256]{2,1,0:T(8,128)(2,1)}) custom-call(bf16[32,8,256]{2,1,0:T(8,128)(2,1)} %get-tuple-element.46.halo, bf16[32,8,256]{2,1,0:T(8,128)(2,1)} %get-tuple-element.47.terms_s, bf16[32,8,256]{2,1,0:T(8,128)(2,1)} %get-tuple-element.48.terms_n, ...), custom_call_target="tpu_custom_call" | custom-call | tf_op jit(solution)/shard_map/pallas_call | solution.py:103
  143.0 3.9 %shard_map.197 = (f32[2048,256]{1,0:T(8,128)}, f32[256,256]{1,0:T(8,128)}, f32[256,256]{1,0:T(8,128)}, f32[512,256]{1,0:T(8,128)}, f32[1,256]{1,0:T(1,128)}, /*index=5*/f32[1,256]{1,0:T(1,128)}) custom-call(f32[2048,256]{1,0:T(8,128)} %get-tuple-element.45.local, bf16[32,8,256]{2,1,0:T(8,128)(2,1)} %get-tuple-element.50.halo_back, ...), custom_call_target="tpu_custom_call" | custom-call | tf_op jit(solution)/shard_map/pallas_call | solution.py:103
where the time goes:
time: 147 us
  Pallas kernels  143 us (97%)
  local copies, waits for them, and re-layouts  2.81 us (2%)
    pallas_call x9, Pallas kernels, call(): pl.pallas_call(body, out_shape=tuple((jax.ShapeDtypeStruct(s, d) for s, d...  143 us

commit v1 on v0

v1 whole, which is shorter than its diff:
```python
import functools

import jax
import jax.numpy as jnp
from jax import lax
from jax.experimental import pallas as pl
from jax.experimental.pallas import tpu as pltpu
from jax.sharding import PartitionSpec as P

F32 = jnp.float32
BF16 = jnp.bfloat16
F8 = jnp.float8_e4m3fn
VMEM_LIMIT = 60 * 1024 * 1024
NN = (((1,), (0,)), ((), ()))
NT = (((1,), (1,)), ((), ()))
TN = (((0,), (0,)), ((), ()))


def dot(left, right, dims=NN):
    return lax.dot_general(left, right, dims, preferred_element_type=F32)


def column_of(row):
    return jnp.broadcast_to(row, (128, row.shape[1])).T[:, :1]


def row_of(column):
    return jnp.broadcast_to(column, (column.shape[0], 128)).T[:1, :]


def equal_mask(left, right):
    return jnp.where(left == right, 1.0, 0.0).astype(BF16)


def iota(shape, dim):
    return lax.broadcasted_iota(jnp.int32, shape, dim).astype(F32)


class Links:
    def __init__(self, peers, grp):
        self.peers, self.grp = peers, grp
        self.me = lax.axis_index("dom") * grp + lax.axis_index("grp")

    def device(self, peer):
        return {"dom": peer // self.grp, "grp": lax.rem(peer, self.grp)}

    def other(self, step):
        return lax.rem(self.me + step, self.peers)

    def each(self, body):
        def step(i, carry):
            body(self.other(i))
            return carry

        lax.fori_loop(1, self.peers, step, 0)

    def greet(self):
        barrier = pltpu.get_barrier_semaphore()
        self.each(lambda peer: pl.semaphore_signal(
            barrier, inc=1, device_id=self.device(peer), device_id_type=pl.DeviceIdType.MESH))

    def greeted(self):
        pl.semaphore_wait(pltpu.get_barrier_semaphore(), self.peers - 1)

    def copy(self, src, dst, send, recv, peer, slot):
        return pltpu.make_async_remote_copy(
            src_ref=src, dst_ref=dst, send_sem=send.at[peer], recv_sem=recv.at[slot],
            device_id=self.device(peer), device_id_type=pl.DeviceIdType.MESH)

    def start(self, moves):
        def one(peer):
            for pick, dst, send, recv in moves:
                self.copy(pick(peer), dst.at[self.me], send, recv, peer, self.me).start()

        self.each(one)

    def finish(self, moves):
        def one(peer):
            for pick, dst, send, recv in moves:
                copy = self.copy(pick(peer), dst.at[peer], send, recv, peer, peer)
                copy.wait_recv()
                copy.wait_send()

        self.each(one)


def block_of(ref):
    return lambda peer: ref.at[peer]


def whole_of(ref):
    return lambda peer: ref


def sems(peers, count):
    return [pltpu.SemaphoreType.DMA((peers,)) for _ in range(2 * count)]


def call(body, outs, args, scratch=(), collective_id=None, smem=(), limit=VMEM_LIMIT):
    params = dict(vmem_limit_bytes=limit)
    if collective_id is not None:
        params.update(collective_id=collective_id, has_side_effects=True)
    return pl.pallas_call(
        body,
        out_shape=tuple(jax.ShapeDtypeStruct(s, d) for s, d in outs),
        in_specs=[
            pl.BlockSpec(memory_space=pltpu.SMEM if i in smem else pltpu.VMEM)
            for i in range(len(args))
        ],
        out_specs=tuple(pl.BlockSpec(memory_space=pltpu.VMEM) for _ in outs),
        scratch_shapes=list(scratch),
        compiler_params=pltpu.CompilerParams(**params),
    )(*args)


def spread_column(rows, length):
    peers = rows.shape[0]
    spread = jnp.broadcast_to(rows, (peers, length, 128)).reshape(peers * length, 128)
    lane = lax.broadcasted_iota(jnp.int32, spread.shape, 1)
    row = lax.rem(lax.broadcasted_iota(jnp.int32, spread.shape, 0), length)
    return jnp.sum(jnp.where(lane == row, spread, 0.0), axis=1, keepdims=True)


def halo_column(halo, turned):
    halo_len, peers = halo.shape
    turned[...] = jnp.zeros_like(turned)
    turned[:halo_len, :peers] = halo[...].astype(F32)
    return spread_column(turned[...].T[:peers].reshape(peers, 1, 128), halo_len)


def first_exchange(peers, grp, feat, halo, request, wanted, arrived, turned, asked, outgoing, s0, r0, s1, r1):
    links = Links(peers, grp)
    me = links.me
    links.greet()
    nodes = feat.shape[0]
    turned[...] = jnp.zeros_like(turned)
    turned[: request.shape[0], :peers] = request[...].astype(F32)
    asked[...] = turned[...].T[:peers].astype(jnp.int32).reshape(asked.shape)
    index = halo_column(halo, turned)
    pick = equal_mask(index, iota((index.shape[0], nodes), 1))
    outgoing[...] = dot(pick, feat[...]).astype(BF16).reshape(outgoing.shape)
    links.greeted()
    moves = [(block_of(asked), wanted, s0, r0), (block_of(outgoing), arrived, s1, r1)]
    links.start(moves)
    wanted[me] = asked[me]
    arrived[me] = outgoing[me]
    links.finish(moves)


def count_edges(req_len, nodes, block, group, src, dst, count, wanted, counts, total, marks, index, ranks, packs, dense):
    rows, table_rows = counts.shape
    depth = src.shape[0]
    bits = nodes.bit_length() - 1
    total[...] = jnp.zeros_like(total)
    column = spread_column(wanted[...].astype(F32), req_len)
    index[...] = jnp.broadcast_to(column, index.shape)
    high = jnp.floor(column * (1.0 / 128.0))
    low = column - high * 128.0
    lanes = iota((rows, 128), 1)
    seen = dot(equal_mask(high, lanes), equal_mask(low, lanes), TN)[: nodes // 128]
    power = lax.shift_left(jnp.ones(seen.shape, jnp.int32), lax.broadcasted_iota(jnp.int32, seen.shape, 0))
    word = jnp.sum(jnp.where(seen > 0.5, power, 0), axis=0, keepdims=True)
    slot = lax.broadcasted_iota(jnp.int32, src.shape, 0) * 128 + lax.broadcasted_iota(jnp.int32, src.shape, 1)
    live = slot < count[0]
    into = jnp.where(live, dst[...], 0)
    flags = jnp.take_along_axis(
        jnp.broadcast_to(word, src.shape), lax.bitwise_and(into, 127), axis=1, mode="promise_in_bounds")
    flag = lax.bitwise_and(lax.shift_right_logical(flags, lax.shift_right_logical(into, 7)), 1)
    active = jnp.where(live, flag, 0)
    ahead = jnp.where(iota((depth, depth), 1) < iota((depth, depth), 0), 1.0, 0.0).astype(BF16)
    amount = active.astype(F32)
    rank = dot(ahead, amount.astype(BF16))
    ranks[...] = jnp.where(active > 0, rank, -1.0)
    packs[...] = src[...] * nodes + into
    longest = jnp.max(jnp.sum(amount, axis=0, keepdims=True)).astype(jnp.int32)
    spots = iota((8, 128), 0)
    held = [jnp.full((8, 128), -1, jnp.int32) for _ in range(depth // 8)]
    for r in range(depth):
        to = jnp.broadcast_to(ranks[r : r + 1, :], (8, 128))
        value = jnp.broadcast_to(packs[r : r + 1, :], (8, 128))
        for b in range(r // 8 + 1):
            held[b] = jnp.where(to == spots + 8.0 * b, value, held[b])
    for b in range(depth // 8):
        dense[8 * b : 8 * b + 8, :] = held[b]

    ladder = iota((block, 128), 0).astype(BF16)

    @pl.loop(0, (longest + group - 1) // group)
    def _(c):
        highs, lows = [], []
        for k in range(group):
            value = dense[pl.ds(c * group + k, 1), :]
            node = jnp.where(value < 0, -1, lax.bitwise_and(value, nodes - 1)).astype(F32)
            marks[:, k * 128 : k * 128 + 128] = jnp.where(index[...] == node, 1.0, 0.0).astype(F8)
            source = lax.shift_right_arithmetic(value, bits)
            highs.append(lax.shift_right_arithmetic(source, block.bit_length() - 1))
            lows.append(lax.bitwise_and(source, block - 1))

        @pl.loop(0, table_rows // block)
        def _(b):
            hits = []
            for k in range(group):
                here = jnp.where(highs[k] == b, lows[k], -1).astype(F32).astype(BF16)
                hits.append(jnp.where(ladder == here, jnp.array(1, BF16), jnp.array(0, BF16)).astype(F8))
            cols = pl.ds(pl.multiple_of(b * block, block), block)
            total[:, cols] += dot(marks[...], jnp.concatenate(hits, axis=1), NT)

    counts[...] = total[...].astype(BF16)


def middle(
    peers, grp, req_len, chunk, block,
    feat, arrived, counts, wanted, halo, w_self, w_neigh, w_hidden, bias, w_out, ends, labels, weight,
    logits, out, g_s, g_n, g_h, g_b, g_o,
    turned, index, feat_w, agg_w, floor, served, received, picks, upper_lower, sums,
    back_sent, back, hidden_sent, hidden_in, hidden_own, hidden_all,
    small, small_in, grad, node_sent, node_in, node_own, node_all, near, far, returned, halo_back,
    s0, r0, s1, r1, s2, r2, s3, r3, s4, r4, s5, r5, s6, r6, s7, r7,
):
    links = Links(peers, grp)
    me = links.me
    nodes, width = feat.shape
    rows, table_rows = counts.shape
    size, parts = row_blocks(rows)
    links.greet()
    index[...] = jnp.broadcast_to(spread_column(wanted[...].astype(F32), req_len), index.shape)
    per = size // req_len
    for i in range(parts):
        span = slice(i * size, i * size + size)
        degree = jnp.sum(counts[span, :].astype(F32), axis=1, keepdims=True)
        floor_deg = jnp.maximum(degree, 1.0)
        total = dot(counts[span, :nodes], feat[...])
        total += dot(counts[span, nodes:], arrived[...].reshape(table_rows - nodes, width))
        agg = (total / floor_deg).astype(BF16)
        own = dot(equal_mask(index[span, :1], iota((size, nodes), 1)), feat[...]).astype(BF16)
        emb = (dot(own, w_self[...]) + dot(agg, w_neigh[...])).astype(BF16)
        served[i * per : i * per + per] = emb.reshape(per, req_len, width)
        feat_w[span, :] = own
        agg_w[span, :] = agg
        floor[span, :] = jnp.broadcast_to(floor_deg, (size, 128))
    links.greeted()
    serve = [(block_of(served), received, s0, r0)]
    links.start(serve)
    received[me] = served[me]
    pairs = ends.shape[1]
    slots = iota((rows, chunk), 0)

    @pl.loop(0, pairs // chunk)
    def _(c):
        span = pl.ds(pl.multiple_of(c * chunk, chunk), chunk)
        end = ends[:, span].astype(F32)
        picks[:rows, span] = equal_mask(slots, end[:1, :])
        picks[rows:, span] = equal_mask(slots, end[1:, :])

    bias_col = column_of(bias[...])
    out_col = column_of(w_out[...])
    sums[...] = jnp.zeros_like(sums)
    links.finish(serve)

    got = received[...].reshape(rows, width)
    for place, half in ((0, w_hidden[:width, :]), (rows, w_hidden[width:, :])):
        exact = dot(got, half).T
        upper = exact.astype(BF16)
        upper_lower[:width, place : place + rows] = upper
        upper_lower[width:, place : place + rows] = (exact - upper.astype(F32)).astype(BF16)

    def step(c, carry):
        bias_sum, out_sum = carry
        span = pl.ds(pl.multiple_of(c * chunk, chunk), chunk)
        both = dot(upper_lower[...], picks[:, span])
        pre = both[:width] + both[width:] + bias_col
        hidden = jnp.maximum(pre, 0.0)
        logit = jnp.sum(hidden * out_col, axis=0, keepdims=True)
        logits[:, span] = logit
        slope = weight[:, span] * (jax.nn.sigmoid(logit) - labels[:, span].astype(F32))
        delta = jnp.where(pre > 0, slope * out_col, 0.0)
        sums[...] += dot(picks[:, span], delta.astype(BF16), NT)
        return (
            bias_sum + jnp.sum(delta, axis=1, keepdims=True),
            out_sum + jnp.sum(hidden * slope, axis=1, keepdims=True),
        )

    zero = jnp.zeros((width, 1), F32)
    bias_sum, out_sum = lax.fori_loop(0, pairs // chunk, step, (zero, zero))
    left = sums[:rows, :].astype(BF16)
    right = sums[rows:, :].astype(BF16)
    back_rows = dot(left, w_hidden[:width, :], NT) + dot(right, w_hidden[width:, :], NT)
    back_sent[...] = back_rows.astype(BF16).reshape(back_sent.shape)
    give = [(block_of(back_sent), back, s1, r1)]
    links.start(give)
    back[me] = back_sent[me]

    small[0:1, :] = row_of(bias_sum)
    small[1:2, :] = row_of(out_sum)
    half = peers // 2
    shape = (half,) + hidden_sent.shape[1:]
    hidden_sent[:half] = dot(got, left, TN).astype(BF16).reshape(shape)
    hidden_sent[half:] = dot(got, right, TN).astype(BF16).reshape(shape)
    hidden_terms = [(block_of(hidden_sent), hidden_in, s2, r2), (whole_of(small), small_in, s3, r3)]
    links.start(hidden_terms)
    hidden_in[me] = hidden_sent[me]
    small_in[me] = small[...]
    other = row_of(index[:, :1])
    links.finish(give)

    for i in range(parts):
        span = slice(i * size, i * size + size)
        same = index[span, :1] == other
        first = lax.broadcasted_iota(jnp.int32, same.shape, 0) + i * size
        earlier = lax.broadcasted_iota(jnp.int32, same.shape, 1) < first
        repeat = jnp.sum(jnp.where(same & earlier, 1.0, 0.0), axis=1, keepdims=True)
        total = dot(jnp.where(same, 1.0, 0.0).astype(BF16), back[...].reshape(rows, width))
        grad[span, :] = jnp.where(repeat > 0.0, 0.0, total).astype(BF16)
    node_sent[:half] = dot(feat_w[...], grad[...], TN).astype(BF16).reshape(shape)
    node_sent[half:] = dot(agg_w[...], grad[...], TN).astype(BF16).reshape(shape)
    node_terms = [(block_of(node_sent), node_in, s4, r4)]
    links.start(node_terms)
    node_in[me] = node_sent[me]

    far[...] = (dot(grad[...], w_neigh[...], NT) / floor[:, :1]).astype(BF16)
    returned[...] = dot(counts[:, nodes:], far[...], TN).astype(BF16).reshape(returned.shape)
    send_back = [(block_of(returned), halo_back, s5, r5)]
    links.start(send_back)
    halo_back[me] = returned[me]

    near[...] = dot(grad[...], w_self[...], NT).astype(BF16)
    links.finish(hidden_terms)
    hidden_own[...] = jnp.sum(hidden_in[...].astype(F32), axis=0).astype(BF16)
    hidden_sums = [(whole_of(hidden_own), hidden_all, s6, r6)]
    links.start(hidden_sums)
    hidden_all[me] = hidden_own[...]

    def local(b, carry):
        cols = pl.ds(pl.multiple_of(b * block, block), block)
        spot = lax.broadcasted_iota(jnp.int32, (1, block), 1) + b * block
        pick = equal_mask(index[:, :1], spot.astype(F32))
        out[cols, :] = dot(counts[:, cols], far[...], TN) + dot(pick, near[...], TN)
        return carry

    lax.fori_loop(0, nodes // block, local, 0)
    links.finish(node_terms)
    node_own[...] = jnp.sum(node_in[...].astype(F32), axis=0).astype(BF16)
    node_sums = [(whole_of(node_own), node_all, s7, r7)]
    links.start(node_sums)
    node_all[me] = node_own[...]

    halo_row = row_of(halo_column(halo, turned))
    links.finish(send_back)

    def add(b, carry):
        cols = pl.ds(pl.multiple_of(b * block, block), block)
        spot = iota((block, halo_row.shape[1]), 0) + (b * block).astype(F32)
        out[cols, :] += dot(equal_mask(spot, halo_row), halo_back[...].reshape(halo_row.shape[1], width))
        return carry

    lax.fori_loop(0, nodes // block, add, 0)
    total = jnp.sum(small_in[...], axis=0)
    g_b[...] = total[0:1, :]
    g_o[...] = total[1:2, :]
    links.finish(hidden_sums)
    g_h[...] = hidden_all[...].astype(F32).reshape(g_h.shape)
    links.finish(node_sums)
    g_s[...] = node_all[:half].astype(F32).reshape(g_s.shape)
    g_n[...] = node_all[half:].astype(F32).reshape(g_n.shape)


def row_blocks(rows):
    size = min(rows, 512)
    return size, rows // size


def per_device(
    features, edge_src, edge_dst, edge_count, halo_index, request_rows, pair_ends,
    labels, pair_weight, w_self, w_neigh, w_hidden, b_hidden, w_out,
):
    nodes, width = features.shape
    grp = lax.axis_size("grp")
    peers = lax.axis_size("dom") * grp
    halo_len = halo_index.shape[2]
    req_len = request_rows.shape[2]
    slots = edge_src.shape[0]
    pairs = labels.shape[0]
    table_rows = nodes + peers * halo_len
    rows = peers * req_len
    block = 256
    part = 2 * width // peers
    turn = max(128, peers)

    halo = halo_index[0].T
    wanted, arrived = call(
        functools.partial(first_exchange, peers, grp),
        [((peers, 1, 128), jnp.int32), ((peers, halo_len, width), BF16)],
        (features, halo, request_rows[0].T),
        [
            pltpu.VMEM((128, turn), F32),
            pltpu.VMEM((peers, 1, 128), jnp.int32),
            pltpu.VMEM((peers, halo_len, width), BF16),
        ] + sems(peers, 2),
        collective_id=0,
    )
    group = 8
    depth = slots // 128
    (counts,) = call(
        functools.partial(count_edges, req_len, nodes, block, group),
        [((rows, table_rows), BF16)],
        (edge_src.reshape(depth, 128), edge_dst.reshape(depth, 128), edge_count, wanted),
        [
            pltpu.VMEM((rows, table_rows), F32),
            pltpu.VMEM((rows, group * 128), F8),
            pltpu.VMEM((rows, 128), F32),
            pltpu.VMEM((depth, 128), F32),
            pltpu.VMEM((depth, 128), jnp.int32),
            pltpu.VMEM((depth, 128), jnp.int32),
        ],
        smem=(2,),
    )
    chunk = 512
    rows_of = lambda *shape: pltpu.VMEM(shape, BF16)
    logits, grad_features, g_s, g_n, g_h, g_b, g_o = call(
        functools.partial(middle, peers, grp, req_len, chunk, block),
        [
            ((1, pairs), F32),
            ((nodes, width), F32),
            ((width, width), F32),
            ((width, width), F32),
            ((2 * width, width), F32),
            ((1, width), F32),
            ((1, width), F32),
        ],
        (
            features, arrived, counts, wanted, halo, w_self, w_neigh, w_hidden,
            b_hidden.reshape(1, width), w_out.reshape(1, width),
            pair_ends.T, labels.reshape(1, pairs), pair_weight.reshape(1, pairs),
        ),
        [
            pltpu.VMEM((128, turn), F32),
            pltpu.VMEM((rows, 128), F32),
            rows_of(rows, width),
            rows_of(rows, width),
            pltpu.VMEM((rows, 128), F32),
            rows_of(peers, req_len, width),
            rows_of(peers, req_len, width),
            rows_of(2 * rows, pairs),
            rows_of(2 * width, 2 * rows),
            pltpu.VMEM((2 * rows, width), F32),
            rows_of(peers, req_len, width),
            rows_of(peers, req_len, width),
            rows_of(peers, part, width),
            rows_of(peers, part, width),
            rows_of(part, width),
            rows_of(peers, part, width),
            pltpu.VMEM((2, width), F32),
            pltpu.VMEM((peers, 2, width), F32),
            rows_of(rows, width),
            rows_of(peers, part, width),
            rows_of(peers, part, width),
            rows_of(part, width),
            rows_of(peers, part, width),
            rows_of(rows, width),
            rows_of(rows, width),
            rows_of(peers, halo_len, width),
            rows_of(peers, halo_len, width),
        ] + sems(peers, 8),
        collective_id=1,
    )
    return (logits.reshape(pairs), grad_features, g_s, g_n, g_h, g_b.reshape(width), g_o.reshape(width))


def solution(mesh):
    both = ("dom", "grp")
    in_specs = (
        P(both, None), P(both), P(both), P(both), P(both, None, None), P(both, None, None),
        P(both, None), P(both), P(both), P(), P(), P(), P(), P(),
    )
    out_specs = (P(both), P(both, None), P(), P(), P(), P(), P())
    return jax.shard_map(
        per_device, mesh=mesh, in_specs=in_specs, out_specs=out_specs, check_vma=False
    )
```

time: 147 us -> 107 us (0.73)
  Pallas kernels: 143 us -> 97.2 us
  local copies, waits for them, and re-layouts: 2.81 us -> 7.77 us
    pallas_call x9 -> x3, Pallas kernels: 143 us -> 97.2 us  [call(): pl.pallas_call(body, out_shape=tuple((jax.ShapeDtypeStruct(s, d) for s, d...]
    unnamed x2 -> x17, local copies, waits for them, and re-layouts: 1.53 us -> 7.77 us
where the time goes in v1:
time: 107 us; the launch traced here: 106 us
  Pallas kernels  97.2 us (91%)
  local copies, waits for them, and re-layouts  7.77 us (7%)
  between operations  1.3 us (1%)
    pallas_call x3, Pallas kernels, call(): pl.pallas_call(body, out_shape=tuple((jax.ShapeDtypeStruct(s, d) for s, d...  97.2 us
    unnamed x17, local copies, waits for them, and re-layouts  7.77 us

profile of v1, /device:TPU:0, one launch (start us, length us, event | category | flops | bytes accessed | tf_op | source)
XLA Modules:
  0.0 106.3 jit_solution(13669428364237574374)
XLA Ops:
  1.3 15.1 %shard_map.189 = (s32[32,1,128]{2,1,0:T(1,128)}, bf16[32,8,256]{2,1,0:T(8,128)(2,1)}) custom-call(bf16[2048,256]{1,0:T(8,128)(2,1)} %feat.3, s32[8,32]{1,0:T(8,128)} %bitcast.19, s32[16,32]{1,0:T(8,128)} %bitcast.21), custom_call_target="tpu_custom_call" | custom-call | tf_op jit(solution)/shard_map/pallas_call | solution.py:103
  16.3 20.7 %shard_map.190.counts = bf16[512,2304]{1,0:T(8,128)(2,1)} custom-call(s32[128,128]{1,0:T(8,128)} %bitcast.16, s32[128,128]{1,0:T(8,128)} %bitcast.17, s32[1]{0:T(128)S(6)} %copy.28.count, s32[32,1,128]{2,1,0:T(1,128)} %get-tuple-element.17.wanted), custom_call_target="tpu_custom_call" | custom-call | tf_op jit(solution)/shard_map/pallas_call | solution.py:103
  37.0 61.5 %shard_map.191 = (f32[1,2048]{1,0:T(1,128)}, f32[2048,256]{1,0:T(8,128)}, f32[256,256]{1,0:T(8,128)}, f32[256,256]{1,0:T(8,128)}, f32[512,256]{1,0:T(8,128)}, /*index=5*/f32[1,256]{1,0:T(1,128)}, f32[1,256]{1,0:T(1,128)}) custom-call(bf16[2048,256]{1,0:T(8,128)(2,1)} %feat.3, bf16[32,8,256]{2,1,0:T(8,128)(2,1)} %get-tuple-element.16.arrived, ...), custom_call_target="tpu_custom_call" | custom-call | tf_op jit(solution)/shard_map/pallas_call | solution.py:103
  98.5 1.3 %copy.29 = f32[2048]{0:T(1024)} copy(f32[2048]{0:T(1024)} %bitcast.24) | data formatting | bytes 16384
  99.8 0.0 copy-start.2
  99.8 0.0 copy-start.1
  99.8 0.0 copy-start
  99.8 3.1 %copy.30 = f32[2048,256]{1,0:T(8,128)} copy(f32[2048,256]{1,0:T(8,128)} %get-tuple-element.33) | data formatting | bytes 4194304
  103.0 0.0 copy-done.2
  103.0 0.0 copy-start.4
  103.0 0.0 copy-start.3
  103.0 0.7 copy.31
  103.7 0.0 copy-done.1
  103.7 0.7 copy.32
  104.4 0.0 copy-done
  104.4 0.8 copy.33
  105.2 0.0 copy-done.4
  105.2 0.6 copy.34
  105.8 0.0 copy-done.3
  105.8 0.6 copy.35
Async XLA Ops:
  99.8 3.1 %copy-start.2 = (f32[256,256]{1,0:T(8,128)S(1)}, f32[256,256]{1,0:T(8,128)}, u32[]{:S(2)}) copy-start(f32[256,256]{1,0:T(8,128)} %get-tuple-element.34) | copy-start | bytes 786436
  99.8 3.8 %copy-start.1 = (f32[256,256]{1,0:T(8,128)S(1)}, f32[256,256]{1,0:T(8,128)}, u32[]{:S(2)}) copy-start(f32[256,256]{1,0:T(8,128)} %get-tuple-element.35) | copy-start | bytes 786436
  99.8 4.6 %copy-start = (f32[512,256]{1,0:T(8,128)S(1)}, f32[512,256]{1,0:T(8,128)}, u32[]{:S(2)}) copy-start(f32[512,256]{1,0:T(8,128)} %get-tuple-element.36) | copy-start | bytes 1572868
  103.0 2.2 %copy-start.4 = (f32[1,256]{1,0:T(1,128)S(1)}, f32[1,256]{1,0:T(1,128)}, u32[]{:S(2)}) copy-start(f32[1,256]{1,0:T(1,128)} %get-tuple-element.23) | copy-start | bytes 3076
  103.0 2.8 %copy-start.3 = (f32[1,256]{1,0:T(1,128)S(1)}, f32[1,256]{1,0:T(1,128)}, u32[]{:S(2)}) copy-start(f32[1,256]{1,0:T(1,128)} %get-tuple-element.24) | copy-start | bytes 3076

commit v2 on v1

--- a/solution.py
+++ b/solution.py
@@ -11,6 +11,8 @@
 BF16 = jnp.bfloat16
 F8 = jnp.float8_e4m3fn
 VMEM_LIMIT = 60 * 1024 * 1024
+K1LIM = 64 * 1024 * 1024 - 512 * 1024
+GROUP = 8
 NN = (((1,), (0,)), ((), ()))
 NT = (((1,), (1,)), ((), ()))
 TN = (((0,), (0,)), ((), ()))
@@ -84,6 +86,15 @@
         self.each(one)
 
 
+class Line(Links):
+    def __init__(self, axis, peers):
+        self.axis, self.peers = axis, peers
+        self.me = lax.axis_index(axis)
+
+    def device(self, peer):
+        return {self.axis: peer}
+
+
 def block_of(ref):
     return lambda peer: ref.at[peer]
 
@@ -96,7 +107,7 @@
     return [pltpu.SemaphoreType.DMA((peers,)) for _ in range(2 * count)]
 
 
-def call(body, outs, args, scratch=(), collective_id=None, smem=(), limit=VMEM_LIMIT):
+def call(body, outs, args, scratch=(), collective_id=None, hbm=(), limit=VMEM_LIMIT, micros=0):
     params = dict(vmem_limit_bytes=limit)
     if collective_id is not None:
         params.update(collective_id=collective_id, has_side_effects=True)
@@ -104,12 +115,13 @@
         body,
         out_shape=tuple(jax.ShapeDtypeStruct(s, d) for s, d in outs),
         in_specs=[
-            pl.BlockSpec(memory_space=pltpu.SMEM if i in smem else pltpu.VMEM)
+            pl.BlockSpec(memory_space=pltpu.HBM if i in hbm else pltpu.VMEM)
             for i in range(len(args))
         ],
         out_specs=tuple(pl.BlockSpec(memory_space=pltpu.VMEM) for _ in outs),
         scratch_shapes=list(scratch),
         compiler_params=pltpu.CompilerParams(**params),
+        cost_estimate=pl.CostEstimate(flops=micros * 10**9, bytes_accessed=1024, transcendentals=0) if micros else None,
     )(*args)
 
 
@@ -128,16 +140,29 @@
     return spread_column(turned[...].T[:peers].reshape(peers, 1, 128), halo_len)
 
 
-def first_exchange(peers, grp, feat, halo, request, wanted, arrived, turned, asked, outgoing, s0, r0, s1, r1):
+def fetch(pairs, done):
+    return [pltpu.make_async_copy(src, dst, done.at[i]) for i, (src, dst) in enumerate(pairs)]
+
+
+def first_exchange(
+    peers, grp, feat_far, halo_far, request_far, wanted, arrived,
+    feat, halo, request, done, turned, asked, outgoing, s0, r0, s1, r1,
+):
     links = Links(peers, grp)
     me = links.me
+    loads = fetch([(request_far, request), (halo_far, halo), (feat_far, feat)], done)
+    for load in loads:
+        load.start()
     links.greet()
     nodes = feat.shape[0]
+    loads[0].wait()
+    loads[1].wait()
     turned[...] = jnp.zeros_like(turned)
     turned[: request.shape[0], :peers] = request[...].astype(F32)
     asked[...] = turned[...].T[:peers].astype(jnp.int32).reshape(asked.shape)
     index = halo_column(halo, turned)
     pick = equal_mask(index, iota((index.shape[0], nodes), 1))
+    loads[2].wait()
     outgoing[...] = dot(pick, feat[...]).astype(BF16).reshape(outgoing.shape)
     links.greeted()
     moves = [(block_of(asked), wanted, s0, r0), (block_of(outgoing), arrived, s1, r1)]
@@ -147,7 +172,10 @@
     links.finish(moves)
 
 
-def count_edges(req_len, nodes, block, group, src, dst, count, wanted, counts, total, marks, index, ranks, packs, dense):
+def count_edges(req_len, nodes, block, group, unroll, src_far, dst_far, count_far, wanted, counts, src, dst, count, done, total, marks, index, ranks, packs, dense):
+    loads = fetch([(dst_far, dst), (src_far, src), (count_far, count)], done)
+    for load in loads:
+        load.start()
     rows, table_rows = counts.shape
     depth = src.shape[0]
     bits = nodes.bit_length() - 1
@@ -161,7 +189,9 @@
     power = lax.shift_left(jnp.ones(seen.shape, jnp.int32), lax.broadcasted_iota(jnp.int32, seen.shape, 0))
     word = jnp.sum(jnp.where(seen > 0.5, power, 0), axis=0, keepdims=True)
     slot = lax.broadcasted_iota(jnp.int32, src.shape, 0) * 128 + lax.broadcasted_iota(jnp.int32, src.shape, 1)
+    loads[2].wait()
     live = slot < count[0]
+    loads[0].wait()
     into = jnp.where(live, dst[...], 0)
     flags = jnp.take_along_axis(
         jnp.broadcast_to(word, src.shape), lax.bitwise_and(into, 127), axis=1, mode="promise_in_bounds")
@@ -171,6 +201,7 @@
     amount = active.astype(F32)
     rank = dot(ahead, amount.astype(BF16))
     ranks[...] = jnp.where(active > 0, rank, -1.0)
+    loads[1].wait()
     packs[...] = src[...] * nodes + into
     longest = jnp.max(jnp.sum(amount, axis=0, keepdims=True)).astype(jnp.int32)
     spots = iota((8, 128), 0)
@@ -196,28 +227,35 @@
             highs.append(lax.shift_right_arithmetic(source, block.bit_length() - 1))
             lows.append(lax.bitwise_and(source, block - 1))
 
-        @pl.loop(0, table_rows // block)
-        def _(b):
-            hits = []
-            for k in range(group):
-                here = jnp.where(highs[k] == b, lows[k], -1).astype(F32).astype(BF16)
-                hits.append(jnp.where(ladder == here, jnp.array(1, BF16), jnp.array(0, BF16)).astype(F8))
-            cols = pl.ds(pl.multiple_of(b * block, block), block)
-            total[:, cols] += dot(marks[...], jnp.concatenate(hits, axis=1), NT)
+        @pl.loop(0, table_rows // (block * unroll))
+        def _(outer):
+            for inner in range(unroll):
+                b = outer * unroll + inner
+                hits = []
+                for k in range(group):
+                    here = jnp.where(highs[k] == b, lows[k], -1).astype(F32).astype(BF16)
+                    hits.append(jnp.where(ladder == here, jnp.array(1, BF16), jnp.array(0, BF16)).astype(F8))
+                cols = pl.ds(pl.multiple_of(b * block, block), block)
+                total[:, cols] += dot(marks[...], jnp.concatenate(hits, axis=1), NT)
 
     counts[...] = total[...].astype(BF16)
 
 
 def middle(
-    peers, grp, req_len, chunk, block,
+    dom, grp, req_len, chunk, block,
     feat, arrived, counts, wanted, halo, w_self, w_neigh, w_hidden, bias, w_out, ends, labels, weight,
     logits, out, g_s, g_n, g_h, g_b, g_o,
     turned, index, feat_w, agg_w, floor, served, received, picks, upper_lower, sums,
-    back_sent, back, hidden_sent, hidden_in, hidden_own, hidden_all,
-    small, small_in, grad, node_sent, node_in, node_own, node_all, near, far, returned, halo_back,
-    s0, r0, s1, r1, s2, r2, s3, r3, s4, r4, s5, r5, s6, r6, s7, r7,
+    back_sent, back, hidden_sent, hidden_in, hidden_part, hidden_parts, hidden_own, hidden_all,
+    small, small_in, small_part, small_parts,
+    grad, self_sent, self_in, self_part, self_parts, self_own, self_all,
+    neigh_sent, neigh_in, neigh_part, neigh_parts, neigh_own, neigh_all,
+    near, far, returned, halo_back,
+    s0, r0, s1, r1, s2, r2, *marks,
 ):
-    links = Links(peers, grp)
+    plane, line = Line("dom", dom), Line("grp", grp)
+    in_plane, in_line, all_plane = marks[0:8], marks[8:16], marks[16:22]
+    links = Links(dom * grp, grp)
     me = links.me
     nodes, width = feat.shape
     rows, table_rows = counts.shape
@@ -292,15 +330,16 @@
 
     small[0:1, :] = row_of(bias_sum)
     small[1:2, :] = row_of(out_sum)
-    half = peers // 2
+    half = dom // 2
     shape = (half,) + hidden_sent.shape[1:]
     hidden_sent[:half] = dot(got, left, TN).astype(BF16).reshape(shape)
     hidden_sent[half:] = dot(got, right, TN).astype(BF16).reshape(shape)
-    hidden_terms = [(block_of(hidden_sent), hidden_in, s2, r2), (whole_of(small), small_in, s3, r3)]
-    links.start(hidden_terms)
-    hidden_in[me] = hidden_sent[me]
-    small_in[me] = small[...]
+    hidden_first = [(block_of(hidden_sent), hidden_in) + in_plane[0:2], (whole_of(small), small_in) + in_plane[2:4]]
+    plane.start(hidden_first)
+    hidden_in[plane.me] = hidden_sent[plane.me]
+    small_in[plane.me] = small[...]
     other = row_of(index[:, :1])
+    halo_row = row_of(halo_column(halo, turned))
     links.finish(give)
 
     for i in range(parts):
@@ -311,24 +350,30 @@
         repeat = jnp.sum(jnp.where(same & earlier, 1.0, 0.0), axis=1, keepdims=True)
         total = dot(jnp.where(same, 1.0, 0.0).astype(BF16), back[...].reshape(rows, width))
         grad[span, :] = jnp.where(repeat > 0.0, 0.0, total).astype(BF16)
-    node_sent[:half] = dot(feat_w[...], grad[...], TN).astype(BF16).reshape(shape)
-    node_sent[half:] = dot(agg_w[...], grad[...], TN).astype(BF16).reshape(shape)
-    node_terms = [(block_of(node_sent), node_in, s4, r4)]
-    links.start(node_terms)
-    node_in[me] = node_sent[me]
+    self_sent[...] = dot(feat_w[...], grad[...], TN).astype(BF16).reshape(self_sent.shape)
+    self_first = [(block_of(self_sent), self_in) + in_plane[4:6]]
+    plane.start(self_first)
+    neigh_sent[...] = dot(agg_w[...], grad[...], TN).astype(BF16).reshape(neigh_sent.shape)
+    neigh_first = [(block_of(neigh_sent), neigh_in) + in_plane[6:8]]
+    plane.start(neigh_first)
+    self_in[plane.me] = self_sent[plane.me]
+    neigh_in[plane.me] = neigh_sent[plane.me]
 
     far[...] = (dot(grad[...], w_neigh[...], NT) / floor[:, :1]).astype(BF16)
     returned[...] = dot(counts[:, nodes:], far[...], TN).astype(BF16).reshape(returned.shape)
-    send_back = [(block_of(returned), halo_back, s5, r5)]
+    send_back = [(block_of(returned), halo_back, s2, r2)]
     links.start(send_back)
     halo_back[me] = returned[me]
 
+    plane.finish(hidden_first)
+    hidden_part[...] = jnp.sum(hidden_in[...].astype(F32), axis=0).astype(BF16)
+    small_part[...] = jnp.sum(small_in[...], axis=0)
+    hidden_next = [(whole_of(hidden_part), hidden_parts) + in_line[0:2], (whole_of(small_part), small_parts) + in_line[2:4]]
+    line.start(hidden_next)
+    hidden_parts[line.me] = hidden_part[...]
+    small_parts[line.me] = small_part[...]
+
     near[...] = dot(grad[...], w_self[...], NT).astype(BF16)
-    links.finish(hidden_terms)
-    hidden_own[...] = jnp.sum(hidden_in[...].astype(F32), axis=0).astype(BF16)
-    hidden_sums = [(whole_of(hidden_own), hidden_all, s6, r6)]
-    links.start(hidden_sums)
-    hidden_all[me] = hidden_own[...]
 
     def local(b, carry):
         cols = pl.ds(pl.multiple_of(b * block, block), block)
@@ -338,13 +383,38 @@
         return carry
 
     lax.fori_loop(0, nodes // block, local, 0)
-    links.finish(node_terms)
-    node_own[...] = jnp.sum(node_in[...].astype(F32), axis=0).astype(BF16)
-    node_sums = [(whole_of(node_own), node_all, s7, r7)]
-    links.start(node_sums)
-    node_all[me] = node_own[...]
-
-    halo_row = row_of(halo_column(halo, turned))
+
+    plane.finish(self_first)
+    self_part[...] = jnp.sum(self_in[...].astype(F32), axis=0).astype(BF16)
+    self_next = [(whole_of(self_part), self_parts) + in_line[4:6]]
+    line.start(self_next)
+    self_parts[line.me] = self_part[...]
+    plane.finish(neigh_first)
+    neigh_part[...] = jnp.sum(neigh_in[...].astype(F32), axis=0).astype(BF16)
+    neigh_next = [(whole_of(neigh_part), neigh_parts) + in_line[6:8]]
+    line.start(neigh_next)
+    neigh_parts[line.me] = neigh_part[...]
+
+    line.finish(hidden_next)
+    hidden_own[...] = jnp.sum(hidden_parts[...].astype(F32), axis=0).astype(BF16)
+    hidden_last = [(whole_of(hidden_own), hidden_all) + all_plane[0:2]]
+    plane.start(hidden_last)
+    hidden_all[plane.me] = hidden_own[...]
+    total = jnp.sum(small_parts[...], axis=0)
+    g_b[...] = total[0:1, :]
+    g_o[...] = total[1:2, :]
+
+    line.finish(self_next)
+    self_own[...] = jnp.sum(self_parts[...].astype(F32), axis=0).astype(BF16)
+    self_last = [(whole_of(self_own), self_all) + all_plane[2:4]]
+    plane.start(self_last)
+    self_all[plane.me] = self_own[...]
+    line.finish(neigh_next)
+    neigh_own[...] = jnp.sum(neigh_parts[...].astype(F32), axis=0).astype(BF16)
+    neigh_last = [(whole_of(neigh_own), neigh_all) + all_plane[4:6]]
+    plane.start(neigh_last)
+    neigh_all[plane.me] = neigh_own[...]
+
     links.finish(send_back)
 
     def add(b, carry):
@@ -354,14 +424,33 @@
         return carry
 
     lax.fori_loop(0, nodes // block, add, 0)
-    total = jnp.sum(small_in[...], axis=0)
-    g_b[...] = total[0:1, :]
-    g_o[...] = total[1:2, :]
-    links.finish(hidden_sums)
+    plane.finish(hidden_last)
     g_h[...] = hidden_all[...].astype(F32).reshape(g_h.shape)
-    links.finish(node_sums)
-    g_s[...] = node_all[:half].astype(F32).reshape(g_s.shape)
-    g_n[...] = node_all[half:].astype(F32).reshape(g_n.shape)
+    plane.finish(self_last)
+    g_s[...] = self_all[...].astype(F32).reshape(g_s.shape)
+    plane.finish(neigh_last)
+    g_n[...] = neigh_all[...].astype(F32).reshape(g_n.shape)
+
+
+def put_out(count, *refs):
+    sent, kept, done = refs[:count], refs[count : 2 * count], refs[2 * count]
+    copies = [pltpu.make_async_copy(src, dst, done.at[i]) for i, (src, dst) in enumerate(zip(sent, kept))]
+    for copy in copies:
+        copy.start()
+    for copy in copies:
+        copy.wait()
+
+
+def store(values):
+    count = len(values)
+    return pl.pallas_call(
+        functools.partial(put_out, count),
+        out_shape=tuple(jax.ShapeDtypeStruct(v.shape, v.dtype) for v in values),
+        in_specs=[pl.BlockSpec(memory_space=pltpu.VMEM)] * count,
+        out_specs=tuple(pl.BlockSpec(memory_space=pl.ANY) for _ in values),
+        scratch_shapes=[pltpu.SemaphoreType.DMA((count,))],
+        compiler_params=pltpu.CompilerParams(vmem_limit_bytes=8 * 1024 * 1024),
+    )(*values)
 
 
 def row_blocks(rows):
@@ -375,7 +464,8 @@
 ):
     nodes, width = features.shape
     grp = lax.axis_size("grp")
-    peers = lax.axis_size("dom") * grp
+    dom = lax.axis_size("dom")
+    peers = dom * grp
     halo_len = halo_index.shape[2]
     req_len = request_rows.shape[2]
     slots = edge_src.shape[0]
@@ -383,7 +473,7 @@
     table_rows = nodes + peers * halo_len
     rows = peers * req_len
     block = 256
-    part = 2 * width // peers
+    piece = width // dom
     turn = max(128, peers)
 
     halo = halo_index[0].T
@@ -392,19 +482,30 @@
         [((peers, 1, 128), jnp.int32), ((peers, halo_len, width), BF16)],
         (features, halo, request_rows[0].T),
         [
+            pltpu.VMEM((nodes, width), BF16),
+            pltpu.VMEM((halo_len, peers), jnp.int32),
+            pltpu.VMEM((req_len, peers), jnp.int32),
+            pltpu.SemaphoreType.DMA((3,)),
             pltpu.VMEM((128, turn), F32),
             pltpu.VMEM((peers, 1, 128), jnp.int32),
             pltpu.VMEM((peers, halo_len, width), BF16),
         ] + sems(peers, 2),
         collective_id=0,
+        hbm=(0, 1, 2),
+        limit=K1LIM,
+        micros=10,
     )
-    group = 8
+    group = GROUP
     depth = slots // 128
     (counts,) = call(
-        functools.partial(count_edges, req_len, nodes, block, group),
+        functools.partial(count_edges, req_len, nodes, block, group, table_rows // block),
         [((rows, table_rows), BF16)],
         (edge_src.reshape(depth, 128), edge_dst.reshape(depth, 128), edge_count, wanted),
         [
+            pltpu.VMEM((depth, 128), jnp.int32),
+            pltpu.VMEM((depth, 128), jnp.int32),
+            pltpu.SMEM((1,), jnp.int32),
+            pltpu.SemaphoreType.DMA((3,)),
             pltpu.VMEM((rows, table_rows), F32),
             pltpu.VMEM((rows, group * 128), F8),
             pltpu.VMEM((rows, 128), F32),
@@ -412,12 +513,13 @@
             pltpu.VMEM((depth, 128), jnp.int32),
             pltpu.VMEM((depth, 128), jnp.int32),
         ],
-        smem=(2,),
+        hbm=(0, 1, 2),
+        limit=min(VMEM_LIMIT, rows * 40 * 1024),
     )
     chunk = 512
     rows_of = lambda *shape: pltpu.VMEM(shape, BF16)
-    logits, grad_features, g_s, g_n, g_h, g_b, g_o = call(
-        functools.partial(middle, peers, grp, req_len, chunk, block),
+    found = call(
+        functools.partial(middle, dom, grp, req_len, chunk, block),
         [
             ((1, pairs), F32),
             ((nodes, width), F32),
@@ -445,24 +547,34 @@
             pltpu.VMEM((2 * rows, width), F32),
             rows_of(peers, req_len, width),
             rows_of(peers, req_len, width),
-            rows_of(peers, part, width),
-            rows_of(peers, part, width),
-            rows_of(part, width),
-            rows_of(peers, part, width),
+            rows_of(dom, 2 * piece, width),
+            rows_of(dom, 2 * piece, width),
+            rows_of(2 * piece, width),
+            rows_of(grp, 2 * piece, width),
+            rows_of(2 * piece, width),
+            rows_of(dom, 2 * piece, width),
             pltpu.VMEM((2, width), F32),
-            pltpu.VMEM((peers, 2, width), F32),
+            pltpu.VMEM((dom, 2, width), F32),
+            pltpu.VMEM((2, width), F32),
+            pltpu.VMEM((grp, 2, width), F32),
             rows_of(rows, width),
-            rows_of(peers, part, width),
-            rows_of(peers, part, width),
-            rows_of(part, width),
-            rows_of(peers, part, width),
+        ] + 2 * [
+            rows_of(dom, piece, width),
+            rows_of(dom, piece, width),
+            rows_of(piece, width),
+            rows_of(grp, piece, width),
+            rows_of(piece, width),
+            rows_of(dom, piece, width),
+        ] + [
             rows_of(rows, width),
             rows_of(rows, width),
             rows_of(peers, halo_len, width),
             rows_of(peers, halo_len, width),
-        ] + sems(peers, 8),
+        ] + sems(peers, 3) + sems(dom, 4) + sems(grp, 4) + sems(dom, 3),
         collective_id=1,
+        limit=min(VMEM_LIMIT, rows * 60 * 1024),
     )
+    logits, grad_features, g_s, g_n, g_h, g_b, g_o = store(found)
     return (logits.reshape(pairs), grad_features, g_s, g_n, g_h, g_b.reshape(width), g_o.reshape(width))
 
 

time: 107 us -> 74.3 us (0.69)
  Pallas kernels: 97.2 us -> 71.5 us
  local copies, waits for them, and re-layouts: 7.77 us -> 0.89 us
    pallas_call x3, Pallas kernels: 97.2 us -> 69.8 us  [call(): pl.pallas_call(body, out_shape=tuple((jax.ShapeDtypeStruct(s, d) for s, d...]
    unnamed x17 -> x30, local copies, waits for them, and re-layouts: 7.77 us -> 0.89 us
    pallas_call x0 -> x1, Pallas kernels: none -> 1.73 us  [store(): pl.pallas_call(functools.partial(put_out, count), out_shape=tuple((jax.Sh...]
where the time goes in v2:
time: 74.3 us; the launch traced here: 73.9 us
  Pallas kernels  71.5 us (96%)
  between operations  1.53 us (2%)
  local copies, waits for them, and re-layouts  0.89 us (1%)
    pallas_call x3, Pallas kernels, call(): pl.pallas_call(body, out_shape=tuple((jax.ShapeDtypeStruct(s, d) for s, d...  69.8 us
    pallas_call x1, Pallas kernels, store(): pl.pallas_call(functools.partial(put_out, count), out_shape=tuple((jax.Sh...  1.73 us

profile of v2, /device:TPU:0, one launch (start us, length us, event | category | flops | bytes accessed | tf_op | source)
XLA Modules:
  0.0 73.9 jit_solution(10287215578833672919)
XLA Ops:
  1.3 0.0 copy-start.7
  1.3 0.0 copy-start.8
  1.3 0.0 copy-start.9
  1.3 0.0 copy-start.10
  1.3 0.0 copy-start.11
  1.3 0.0 copy-start.12
  1.3 0.0 copy-start.13
  1.4 0.0 copy-start.14
  1.4 14.1 %shard_map.189 = (s32[32,1,128]{2,1,0:T(1,128)}, bf16[32,8,256]{2,1,0:T(8,128)(2,1)}) custom-call(bf16[2048,256]{1,0:T(8,128)(2,1)} %feat.1, s32[8,32]{1,0:T(8,128)} %bitcast.21, s32[16,32]{1,0:T(8,128)} %bitcast.25), custom_call_target="tpu_custom_call" | custom-call | flops 10000000000 | bytes 1024 | tf_op jit(solution)/shard_map/pallas_call | solution.py:114
  15.4 0.0 copy-start
  15.4 0.0 copy-start.1
  15.5 0.0 copy-start.2
  15.5 0.0 copy-start.3
  15.5 0.0 copy-start.4
  15.5 0.0 copy-done.7
  15.5 0.0 copy-done.8
  15.5 0.8 %copy-done.5 = s32[32,1,128]{2,1,0:T(1,128)S(1)} copy-done((s32[32,1,128]{2,1,0:T(1,128)S(1)}, s32[32,1,128]{2,1,0:T(1,128)}, u32[]{:S(2)}) %copy-start.5) | copy-done | bytes 16408
  16.3 10.9 %shard_map.190.counts = bf16[512,2304]{1,0:T(8,128)(2,1)S(1)} custom-call(s32[128,128]{1,0:T(8,128)S(1)} %bitcast.16, s32[128,128]{1,0:T(8,128)S(1)} %bitcast.17, s32[1]{0:T(128)S(6)} %copy.21.count_far, s32[32,1,128]{2,1,0:T(1,128)S(1)} %copy-done.5), custom_call_target="tpu_custom_call" | custom-call | tf_op jit(solution)/shard_map/pallas_call | solution.py:114
  27.2 0.0 copy-done.9
  27.2 0.0 copy-done.10
  27.2 0.0 copy-done.11
  27.3 0.0 copy-done.12
  27.3 0.0 copy-done.13
  27.3 0.0 copy-done.14
  27.3 0.0 copy-done
  27.3 0.0 copy-done.1
  27.3 0.0 copy-done.2
  27.3 0.0 copy-done.3
  27.3 0.0 copy-done.4
  27.3 0.0 copy-done.6
  27.3 44.8 %shard_map.191 = (f32[1,2048]{1,0:T(1,128)S(1)}, f32[2048,256]{1,0:T(8,128)S(1)}, f32[256,256]{1,0:T(8,128)S(1)}, f32[256,256]{1,0:T(8,128)S(1)}, f32[512,256]{1...) custom-call(bf16[2048,256]{1,0:T(8,128)(2,1)S(1)} %copy-done, bf16[32,8,256]{2,1,0:T(8,128)(2,1)S(1)} %copy-done.4, ...), custom_call_target="tpu_custom_call" | custom-call | tf_op jit(solution)/shard_map/pallas_call | solution.py:114
  72.2 1.7 %shard_map.192 = (f32[1,2048]{1,0:T(1,128)}, f32[2048,256]{1,0:T(8,128)}, f32[256,256]{1,0:T(8,128)}, f32[256,256]{1,0:T(8,128)}, f32[512,256]{1,0:T(8,128)}, /*index=5*/f32[1,256]{1,0:T(1,128)}, f32[1,256]{1,0:T(1,128)}) custom-call(f32[1,2048]{1,0:T(1,128)S(1)} %get-tuple-element.25.refs_0_, f32[2048,256]{1,0:T(8,128)S(1)} %get-tuple-element.26.refs_1_, ...), custom_call_target="tpu_custom_call" | custom-call | tf_op jit(solution)/shard_map/pallas_call | solution.py:446
  (2 shorter events, 0.0 us)
Async XLA Ops:
  1.3 14.2 %copy-start.7 = (s32[16384]{0:T(1024)S(1)}, s32[16384]{0:T(1024)}, u32[]{:S(2)}) copy-start(s32[16384]{0:T(1024)} %param.15) | copy-start | bytes 196612
  1.3 14.2 %copy-start.8 = (s32[16384]{0:T(1024)S(1)}, s32[16384]{0:T(1024)}, u32[]{:S(2)}) copy-start(s32[16384]{0:T(1024)} %param.16) | copy-start | bytes 196612
  1.3 25.9 %copy-start.9 = (s32[2048,2]{0,1:T(2,128)S(1)}, s32[2048,2]{0,1:T(2,128)}, u32[]{:S(2)}) copy-start(s32[2048,2]{0,1:T(2,128)} %param.20) | copy-start | bytes 49156
  1.3 25.9 %copy-start.10 = (s32[2048]{0:T(1024)S(1)}, s32[2048]{0:T(1024)}, u32[]{:S(2)}) copy-start(s32[2048]{0:T(1024)} %param.21) | copy-start | bytes 24580
  1.3 25.9 %copy-start.11 = (f32[2048]{0:T(1024)S(1)}, f32[2048]{0:T(1024)}, u32[]{:S(2)}) copy-start(f32[2048]{0:T(1024)} %param.22) | copy-start | bytes 24580
  1.3 25.9 %copy-start.12 = (s32[1,32,8]{1,2,0:T(8,128)S(1)}, s32[1,32,8]{1,2,0:T(8,128)}, u32[]{:S(2)}) copy-start(s32[1,32,8]{1,2,0:T(8,128)} %param.18) | copy-start | bytes 3076
  1.3 25.9 %copy-start.13 = (f32[256]{0:T(256)S(1)}, f32[256]{0:T(256)}, u32[]{:S(2)}) copy-start(f32[256]{0:T(256)} %param.26) | copy-start | bytes 3076
  1.4 25.9 %copy-start.14 = (f32[256]{0:T(256)S(1)}, f32[256]{0:T(256)}, u32[]{:S(2)}) copy-start(f32[256]{0:T(256)} %param.27) | copy-start | bytes 3076
  15.4 11.9 %copy-start = (bf16[2048,256]{1,0:T(8,128)(2,1)S(1)}, bf16[2048,256]{1,0:T(8,128)(2,1)}, u32[]{:S(2)}) copy-start(bf16[2048,256]{1,0:T(8,128)(2,1)} %feat.1) | copy-start | bytes 3145732
  15.4 11.8 %copy-start.1 = (bf16[512,256]{1,0:T(8,128)(2,1)S(1)}, bf16[512,256]{1,0:T(8,128)(2,1)}, u32[]{:S(2)}) copy-start(bf16[512,256]{1,0:T(8,128)(2,1)} %w_hidden.1) | copy-start | bytes 786436
  15.5 11.8 %copy-start.2 = (bf16[256,256]{1,0:T(8,128)(2,1)S(1)}, bf16[256,256]{1,0:T(8,128)(2,1)}, u32[]{:S(2)}) copy-start(bf16[256,256]{1,0:T(8,128)(2,1)} %w_self.1) | copy-start | bytes 393220
  15.5 11.8 %copy-start.3 = (bf16[256,256]{1,0:T(8,128)(2,1)S(1)}, bf16[256,256]{1,0:T(8,128)(2,1)}, u32[]{:S(2)}) copy-start(bf16[256,256]{1,0:T(8,128)(2,1)} %w_neigh.1) | copy-start | bytes 393220
  15.5 11.8 %copy-start.4 = (bf16[32,8,256]{2,1,0:T(8,128)(2,1)S(1)}, bf16[32,8,256]{2,1,0:T(8,128)(2,1)}, u32[]{:S(2)}) copy-start(bf16[32,8,256]{2,1,0:T(8,128)(2,1)} %get-tuple-element.23.arrived) | copy-start | bytes 393220
  15.5 0.8 %copy-start.5 = (s32[32,1,128]{2,1,0:T(1,128)S(1)}, s32[32,1,128]{2,1,0:T(1,128)}, u32[]{:S(2)}) copy-start(s32[32,1,128]{2,1,0:T(1,128)} %get-tuple-element.24.wanted) | copy-start | bytes 49156
  16.3 11.0 %copy-start.6 = (s32[32,1,128]{2,1,0:T(1,128)S(1)}, s32[32,1,128]{2,1,0:T(1,128)}, u32[]{:S(2)}) copy-start(s32[32,1,128]{2,1,0:T(1,128)} %get-tuple-element.24.wanted) | copy-start | bytes 49156

commit v3 on v2

--- a/solution.py
+++ b/solution.py
@@ -10,9 +10,8 @@
 F32 = jnp.float32
 BF16 = jnp.bfloat16
 F8 = jnp.float8_e4m3fn
-VMEM_LIMIT = 60 * 1024 * 1024
+VMEM_LIMIT = 63 * 1024 * 1024
 K1LIM = 64 * 1024 * 1024 - 512 * 1024
-GROUP = 8
 NN = (((1,), (0,)), ((), ()))
 NT = (((1,), (1,)), ((), ()))
 TN = (((0,), (0,)), ((), ()))
@@ -172,13 +171,35 @@
     links.finish(moves)
 
 
-def count_edges(req_len, nodes, block, group, unroll, src_far, dst_far, count_far, wanted, counts, src, dst, count, done, total, marks, index, ranks, packs, dense):
+def mark_edges(values, index, marks, nodes, block):
+    highs, lows = [], []
+    for k, value in enumerate(values):
+        node = jnp.where(value < 0, -1, lax.bitwise_and(value, nodes - 1)).astype(F32)
+        marks[:, k * 128 : k * 128 + 128] = jnp.where(index[...] == node, 1.0, 0.0).astype(F8)
+        source = lax.shift_right_arithmetic(value, nodes.bit_length() - 1)
+        highs.append(lax.shift_right_arithmetic(source, block.bit_length() - 1))
+        lows.append(lax.bitwise_and(source, block - 1))
+    ladder = iota((block, 128), 0).astype(BF16)
+
+    def count(b):
+        hits = []
+        for high, low in zip(highs, lows):
+            here = jnp.where(high == b, low, -1).astype(F32).astype(BF16)
+            hits.append(jnp.where(ladder == here, jnp.array(1, BF16), jnp.array(0, BF16)).astype(F8))
+        return dot(marks[...], jnp.concatenate(hits, axis=1), NT)
+
+    return count
+
+
+def count_edges(
+    req_len, nodes, block, group, merge, early, src_far, dst_far, count_far, wanted, counts, head,
+    src, dst, count, done, total, marks, index, ranks, packs, dense,
+):
     loads = fetch([(dst_far, dst), (src_far, src), (count_far, count)], done)
     for load in loads:
         load.start()
     rows, table_rows = counts.shape
     depth = src.shape[0]
-    bits = nodes.bit_length() - 1
     total[...] = jnp.zeros_like(total)
     column = spread_column(wanted[...].astype(F32), req_len)
     index[...] = jnp.broadcast_to(column, index.shape)
@@ -188,7 +209,8 @@
     seen = dot(equal_mask(high, lanes), equal_mask(low, lanes), TN)[: nodes // 128]
     power = lax.shift_left(jnp.ones(seen.shape, jnp.int32), lax.broadcasted_iota(jnp.int32, seen.shape, 0))
     word = jnp.sum(jnp.where(seen > 0.5, power, 0), axis=0, keepdims=True)
-    slot = lax.broadcasted_iota(jnp.int32, src.shape, 0) * 128 + lax.broadcasted_iota(jnp.int32, src.shape, 1)
+    lane = lax.broadcasted_iota(jnp.int32, src.shape, 1)
+    slot = lax.broadcasted_iota(jnp.int32, src.shape, 0) * 128 + lane
     loads[2].wait()
     live = slot < count[0]
     loads[0].wait()
@@ -196,73 +218,80 @@
     flags = jnp.take_along_axis(
         jnp.broadcast_to(word, src.shape), lax.bitwise_and(into, 127), axis=1, mode="promise_in_bounds")
     flag = lax.bitwise_and(lax.shift_right_logical(flags, lax.shift_right_logical(into, 7)), 1)
-    active = jnp.where(live, flag, 0)
+    active = jnp.where(live, flag, 0).astype(F32)
+    stride = 128 // merge
     ahead = jnp.where(iota((depth, depth), 1) < iota((depth, depth), 0), 1.0, 0.0).astype(BF16)
-    amount = active.astype(F32)
-    rank = dot(ahead, amount.astype(BF16))
-    ranks[...] = jnp.where(active > 0, rank, -1.0)
+    group_sum = active
+    before = jnp.zeros_like(active)
+    for d in range(1, merge):
+        turned = pltpu.roll(active, d * stride, 1)
+        group_sum = group_sum + turned
+        before = before + jnp.where(lane >= d * stride, turned, 0.0)
+    rank = dot(ahead, group_sum.astype(BF16)) + before
+    spot = jnp.floor(rank * (1.0 / merge))
+    moved = rank - spot * merge - (lane // stride).astype(F32)
+    moved = jnp.where(moved < 0.0, moved + merge, moved)
     loads[1].wait()
-    packs[...] = src[...] * nodes + into
-    longest = jnp.max(jnp.sum(amount, axis=0, keepdims=True)).astype(jnp.int32)
-    spots = iota((8, 128), 0)
-    held = [jnp.full((8, 128), -1, jnp.int32) for _ in range(depth // 8)]
-    for r in range(depth):
-        to = jnp.broadcast_to(ranks[r : r + 1, :], (8, 128))
-        value = jnp.broadcast_to(packs[r : r + 1, :], (8, 128))
-        for b in range(r // 8 + 1):
-            held[b] = jnp.where(to == spots + 8.0 * b, value, held[b])
+    pack = src[...] * nodes + into
+    for d in range(merge):
+        goes = jnp.where((active > 0.5) & (moved == d), spot, -1.0)
+        ranks[d] = pltpu.roll(goes, d * stride, 1) if d else goes
+        packs[d] = pltpu.roll(pack, d * stride, 1) if d else pack
+    most = jnp.max(jnp.sum(group_sum, axis=0, keepdims=True)).astype(jnp.int32)
+    longest = (most + merge - 1) // merge
+    steps = iota((8, 128), 0)
     for b in range(depth // 8):
-        dense[8 * b : 8 * b + 8, :] = held[b]
-
-    ladder = iota((block, 128), 0).astype(BF16)
-
-    @pl.loop(0, (longest + group - 1) // group)
+        @pl.when((b * 8 < longest) | (b * 8 < early * group))
+        def _():
+            held = jnp.full((8, 128), -1, jnp.int32)
+            for r in range(8 * b, depth):
+                for d in range(merge):
+                    to = jnp.broadcast_to(ranks[d, r : r + 1, :], (8, 128))
+                    value = jnp.broadcast_to(packs[d, r : r + 1, :], (8, 128))
+                    held = jnp.where(to == steps + 8.0 * b, value, held)
+            dense[8 * b : 8 * b + 8, :] = held
+    head[...] = dense[: head.shape[0], :]
+
+    @pl.loop(early, (longest + group - 1) // group)
     def _(c):
-        highs, lows = [], []
-        for k in range(group):
-            value = dense[pl.ds(c * group + k, 1), :]
-            node = jnp.where(value < 0, -1, lax.bitwise_and(value, nodes - 1)).astype(F32)
-            marks[:, k * 128 : k * 128 + 128] = jnp.where(index[...] == node, 1.0, 0.0).astype(F8)
-            source = lax.shift_right_arithmetic(value, bits)
-            highs.append(lax.shift_right_arithmetic(source, block.bit_length() - 1))
-            lows.append(lax.bitwise_and(source, block - 1))
-
-        @pl.loop(0, table_rows // (block * unroll))
-        def _(outer):
-            for inner in range(unroll):
-                b = outer * unroll + inner
-                hits = []
-                for k in range(group):
-                    here = jnp.where(highs[k] == b, lows[k], -1).astype(F32).astype(BF16)
-                    hits.append(jnp.where(ladder == here, jnp.array(1, BF16), jnp.array(0, BF16)).astype(F8))
-                cols = pl.ds(pl.multiple_of(b * block, block), block)
-                total[:, cols] += dot(marks[...], jnp.concatenate(hits, axis=1), NT)
+        values = [dense[pl.ds(c * group + k, 1), :] for k in range(group)]
+        count_block = mark_edges(values, index, marks, nodes, block)
+        for b in range(table_rows // block):
+            total[:, b * block : b * block + block] += count_block(b)
 
     counts[...] = total[...].astype(BF16)
 
 
 def middle(
-    dom, grp, req_len, chunk, block,
-    feat, arrived, counts, wanted, halo, w_self, w_neigh, w_hidden, bias, w_out, ends, labels, weight,
+    dom, grp, req_len, chunk, block, early,
+    feat, arrived, counted, head, wanted, halo, w_self, w_neigh, w_hidden, bias, w_out, ends, labels, weight,
     logits, out, g_s, g_n, g_h, g_b, g_o,
-    turned, index, feat_w, agg_w, floor, served, received, picks, upper_lower, sums,
-    back_sent, back, hidden_sent, hidden_in, hidden_part, hidden_parts, hidden_own, hidden_all,
+    turned, index, feat_w, agg_w, floor, served, received, picks, upper_lower, deltas,
+    back_sent, back, hidden_sent, hidden_in, hidden_part, hidden_pieces, hidden_piece, hidden_own, hidden_all,
     small, small_in, small_part, small_parts,
     grad, self_sent, self_in, self_part, self_parts, self_own, self_all,
     neigh_sent, neigh_in, neigh_part, neigh_parts, neigh_own, neigh_all,
-    near, far, returned, halo_back,
-    s0, r0, s1, r1, s2, r2, *marks,
+    near, far, returned, halo_back, feat_t, agg_t,
+    s0, r0, s1, r1, s2, r2, *more,
 ):
     plane, line = Line("dom", dom), Line("grp", grp)
-    in_plane, in_line, all_plane = marks[0:8], marks[8:16], marks[16:22]
+    in_plane, in_line, all_plane, extra = more[0:8], more[8:18], more[18:24], more[24:]
     links = Links(dom * grp, grp)
     me = links.me
     nodes, width = feat.shape
-    rows, table_rows = counts.shape
+    rows, table_rows = counted.shape
     size, parts = row_blocks(rows)
     links.greet()
     index[...] = jnp.broadcast_to(spread_column(wanted[...].astype(F32), req_len), index.shape)
     per = size // req_len
+    counts = counted
+    if early:
+        counts, edge_marks = extra
+        values = [head[k : k + 1, :] for k in range(head.shape[0])]
+        count_block = mark_edges(values, index, edge_marks, nodes, block)
+        for b in range(table_rows // block):
+            cols = slice(b * block, b * block + block)
+            counts[:, cols] = (counted[:, cols].astype(F32) + count_block(b)).astype(BF16)
     for i in range(parts):
         span = slice(i * size, i * size + size)
         degree = jnp.sum(counts[span, :].astype(F32), axis=1, keepdims=True)
@@ -292,7 +321,6 @@
 
     bias_col = column_of(bias[...])
     out_col = column_of(w_out[...])
-    sums[...] = jnp.zeros_like(sums)
     links.finish(serve)
 
     got = received[...].reshape(rows, width)
@@ -312,16 +340,16 @@
         logits[:, span] = logit
         slope = weight[:, span] * (jax.nn.sigmoid(logit) - labels[:, span].astype(F32))
         delta = jnp.where(pre > 0, slope * out_col, 0.0)
-        sums[...] += dot(picks[:, span], delta.astype(BF16), NT)
+        deltas[:, span] = delta.astype(BF16)
         return (
             bias_sum + jnp.sum(delta, axis=1, keepdims=True),
             out_sum + jnp.sum(hidden * slope, axis=1, keepdims=True),
         )
 
     zero = jnp.zeros((width, 1), F32)
-    bias_sum, out_sum = lax.fori_loop(0, pairs // chunk, step, (zero, zero))
-    left = sums[:rows, :].astype(BF16)
-    right = sums[rows:, :].astype(BF16)
+    bias_sum, out_sum = lax.fori_loop(0, pairs // chunk, step, (zero, zero), unroll=True)
+    left = dot(picks[:rows, :], deltas[...], NT).astype(BF16)
+    right = dot(picks[rows:, :], deltas[...], NT).astype(BF16)
     back_rows = dot(left, w_hidden[:width, :], NT) + dot(right, w_hidden[width:, :], NT)
     back_sent[...] = back_rows.astype(BF16).reshape(back_sent.shape)
     give = [(block_of(back_sent), back, s1, r1)]
@@ -340,39 +368,51 @@
     small_in[plane.me] = small[...]
     other = row_of(index[:, :1])
     halo_row = row_of(halo_column(halo, turned))
+    feat_t[...] = feat_w[...].T
+    agg_t[...] = agg_w[...].T
+    plane.finish(hidden_first)
+    hidden_part[...] = jnp.sum(hidden_in[...].astype(F32), axis=0).astype(BF16).reshape(hidden_part.shape)
+    small_part[...] = jnp.sum(small_in[...], axis=0)
+    hidden_second = [
+        (block_of(hidden_part), hidden_pieces) + in_line[0:2],
+        (whole_of(small_part), small_parts) + in_line[2:4],
+    ]
+    line.start(hidden_second)
+    hidden_pieces[line.me] = hidden_part[line.me]
+    small_parts[line.me] = small_part[...]
     links.finish(give)
 
+    back_all = back[...].reshape(rows, width)
+    self_sent[...] = dot(feat_t[...], back_all).astype(BF16).reshape(self_sent.shape)
+    self_first = [(block_of(self_sent), self_in) + in_plane[4:6]]
+    plane.start(self_first)
+    neigh_sent[...] = dot(agg_t[...], back_all).astype(BF16).reshape(neigh_sent.shape)
+    neigh_first = [(block_of(neigh_sent), neigh_in) + in_plane[6:8]]
+    plane.start(neigh_first)
     for i in range(parts):
         span = slice(i * size, i * size + size)
         same = index[span, :1] == other
         first = lax.broadcasted_iota(jnp.int32, same.shape, 0) + i * size
         earlier = lax.broadcasted_iota(jnp.int32, same.shape, 1) < first
         repeat = jnp.sum(jnp.where(same & earlier, 1.0, 0.0), axis=1, keepdims=True)
-        total = dot(jnp.where(same, 1.0, 0.0).astype(BF16), back[...].reshape(rows, width))
+        total = dot(jnp.where(same, 1.0, 0.0).astype(BF16), back_all)
         grad[span, :] = jnp.where(repeat > 0.0, 0.0, total).astype(BF16)
-    self_sent[...] = dot(feat_w[...], grad[...], TN).astype(BF16).reshape(self_sent.shape)
-    self_first = [(block_of(self_sent), self_in) + in_plane[4:6]]
-    plane.start(self_first)
-    neigh_sent[...] = dot(agg_w[...], grad[...], TN).astype(BF16).reshape(neigh_sent.shape)
-    neigh_first = [(block_of(neigh_sent), neigh_in) + in_plane[6:8]]
-    plane.start(neigh_first)
-    self_in[plane.me] = self_sent[plane.me]
-    neigh_in[plane.me] = neigh_sent[plane.me]
-
     far[...] = (dot(grad[...], w_neigh[...], NT) / floor[:, :1]).astype(BF16)
     returned[...] = dot(counts[:, nodes:], far[...], TN).astype(BF16).reshape(returned.shape)
     send_back = [(block_of(returned), halo_back, s2, r2)]
     links.start(send_back)
     halo_back[me] = returned[me]
-
-    plane.finish(hidden_first)
-    hidden_part[...] = jnp.sum(hidden_in[...].astype(F32), axis=0).astype(BF16)
-    small_part[...] = jnp.sum(small_in[...], axis=0)
-    hidden_next = [(whole_of(hidden_part), hidden_parts) + in_line[0:2], (whole_of(small_part), small_parts) + in_line[2:4]]
-    line.start(hidden_next)
-    hidden_parts[line.me] = hidden_part[...]
-    small_parts[line.me] = small_part[...]
-
+    self_in[plane.me] = self_sent[plane.me]
+    neigh_in[plane.me] = neigh_sent[plane.me]
+
+    line.finish(hidden_second)
+    hidden_piece[...] = jnp.sum(hidden_pieces[...].astype(F32), axis=0).astype(BF16)
+    hidden_third = [(whole_of(hidden_piece), hidden_own) + in_line[4:6]]
+    line.start(hidden_third)
+    hidden_own[line.me] = hidden_piece[...]
+    total = jnp.sum(small_parts[...], axis=0)
+    g_b[...] = total[0:1, :]
+    g_o[...] = total[1:2, :]
     near[...] = dot(grad[...], w_self[...], NT).astype(BF16)
 
     def local(b, carry):
@@ -382,28 +422,34 @@
         out[cols, :] = dot(counts[:, cols], far[...], TN) + dot(pick, near[...], TN)
         return carry
 
-    lax.fori_loop(0, nodes // block, local, 0)
-
+    cut = nodes // block * 5 // 8
+    lax.fori_loop(0, cut, local, 0)
     plane.finish(self_first)
     self_part[...] = jnp.sum(self_in[...].astype(F32), axis=0).astype(BF16)
-    self_next = [(whole_of(self_part), self_parts) + in_line[4:6]]
+    self_next = [(whole_of(self_part), self_parts) + in_line[6:8]]
     line.start(self_next)
     self_parts[line.me] = self_part[...]
+    lax.fori_loop(cut, nodes // block, local, 0)
     plane.finish(neigh_first)
     neigh_part[...] = jnp.sum(neigh_in[...].astype(F32), axis=0).astype(BF16)
-    neigh_next = [(whole_of(neigh_part), neigh_parts) + in_line[6:8]]
+    neigh_next = [(whole_of(neigh_part), neigh_parts) + in_line[8:10]]
     line.start(neigh_next)
     neigh_parts[line.me] = neigh_part[...]
 
-    line.finish(hidden_next)
-    hidden_own[...] = jnp.sum(hidden_parts[...].astype(F32), axis=0).astype(BF16)
+    line.finish(hidden_third)
     hidden_last = [(whole_of(hidden_own), hidden_all) + all_plane[0:2]]
     plane.start(hidden_last)
     hidden_all[plane.me] = hidden_own[...]
-    total = jnp.sum(small_parts[...], axis=0)
-    g_b[...] = total[0:1, :]
-    g_o[...] = total[1:2, :]
-
+
+    links.finish(send_back)
+
+    def add(b, carry):
+        cols = pl.ds(pl.multiple_of(b * block, block), block)
+        spot = iota((block, halo_row.shape[1]), 0) + (b * block).astype(F32)
+        out[cols, :] += dot(equal_mask(spot, halo_row), halo_back[...].reshape(halo_row.shape[1], width))
+        return carry
+
+    lax.fori_loop(0, nodes // block, add, 0)
     line.finish(self_next)
     self_own[...] = jnp.sum(self_parts[...].astype(F32), axis=0).astype(BF16)
     self_last = [(whole_of(self_own), self_all) + all_plane[2:4]]
@@ -414,16 +460,6 @@
     neigh_last = [(whole_of(neigh_own), neigh_all) + all_plane[4:6]]
     plane.start(neigh_last)
     neigh_all[plane.me] = neigh_own[...]
-
-    links.finish(send_back)
-
-    def add(b, carry):
-        cols = pl.ds(pl.multiple_of(b * block, block), block)
-        spot = iota((block, halo_row.shape[1]), 0) + (b * block).astype(F32)
-        out[cols, :] += dot(equal_mask(spot, halo_row), halo_back[...].reshape(halo_row.shape[1], width))
-        return carry
-
-    lax.fori_loop(0, nodes // block, add, 0)
     plane.finish(hidden_last)
     g_h[...] = hidden_all[...].astype(F32).reshape(g_h.shape)
     plane.finish(self_last)
@@ -495,11 +531,13 @@
         limit=K1LIM,
         micros=10,
     )
-    group = GROUP
+    group = 8
     depth = slots // 128
-    (counts,) = call(
-        functools.partial(count_edges, req_len, nodes, block, group, table_rows // block),
-        [((rows, table_rows), BF16)],
+    merge = 2
+    early = 1 if rows <= 1024 else 0
+    counts, head = call(
+        functools.partial(count_edges, req_len, nodes, block, group, merge, early),
+        [((rows, table_rows), BF16), ((group, 128), jnp.int32)],
         (edge_src.reshape(depth, 128), edge_dst.reshape(depth, 128), edge_count, wanted),
         [
             pltpu.VMEM((depth, 128), jnp.int32),
@@ -509,17 +547,18 @@
             pltpu.VMEM((rows, table_rows), F32),
             pltpu.VMEM((rows, group * 128), F8),
             pltpu.VMEM((rows, 128), F32),
-            pltpu.VMEM((depth, 128), F32),
-            pltpu.VMEM((depth, 128), jnp.int32),
+            pltpu.VMEM((merge, depth, 128), F32),
+            pltpu.VMEM((merge, depth, 128), jnp.int32),
             pltpu.VMEM((depth, 128), jnp.int32),
         ],
         hbm=(0, 1, 2),
+        micros=10,
         limit=min(VMEM_LIMIT, rows * 40 * 1024),
     )
     chunk = 512
     rows_of = lambda *shape: pltpu.VMEM(shape, BF16)
     found = call(
-        functools.partial(middle, dom, grp, req_len, chunk, block),
+        functools.partial(middle, dom, grp, req_len, chunk, block, early),
         [
             ((1, pairs), F32),
             ((nodes, width), F32),
@@ -530,7 +569,7 @@
             ((1, width), F32),
         ],
         (
-            features, arrived, counts, wanted, halo, w_self, w_neigh, w_hidden,
+            features, arrived, counts, head, wanted, halo, w_self, w_neigh, w_hidden,
             b_hidden.reshape(1, width), w_out.reshape(1, width),
             pair_ends.T, labels.reshape(1, pairs), pair_weight.reshape(1, pairs),
         ),
@@ -544,15 +583,16 @@
             rows_of(peers, req_len, width),
             rows_of(2 * rows, pairs),
             rows_of(2 * width, 2 * rows),
-            pltpu.VMEM((2 * rows, width), F32),
+            rows_of(width, pairs),
             rows_of(peers, req_len, width),
             rows_of(peers, req_len, width),
             rows_of(dom, 2 * piece, width),
             rows_of(dom, 2 * piece, width),
-            rows_of(2 * piece, width),
-            rows_of(grp, 2 * piece, width),
-            rows_of(2 * piece, width),
-            rows_of(dom, 2 * piece, width),
+            rows_of(grp, 2 * piece // grp, width),
+            rows_of(grp, 2 * piece // grp, width),
+            rows_of(2 * piece // grp, width),
+            rows_of(grp, 2 * piece // grp, width),
+            rows_of(dom, grp, 2 * piece // grp, width),
             pltpu.VMEM((2, width), F32),
             pltpu.VMEM((dom, 2, width), F32),
             pltpu.VMEM((2, width), F32),
@@ -570,7 +610,9 @@
             rows_of(rows, width),
             rows_of(peers, halo_len, width),
             rows_of(peers, halo_len, width),
-        ] + sems(peers, 3) + sems(dom, 4) + sems(grp, 4) + sems(dom, 3),
+            rows_of(width, rows),
+            rows_of(width, rows),
+        ] + sems(peers, 3) + sems(dom, 4) + sems(grp, 5) + sems(dom, 3) + early * [rows_of(rows, table_rows), pltpu.VMEM((rows, group * 128), F8)],
         collective_id=1,
         limit=min(VMEM_LIMIT, rows * 60 * 1024),
     )

time: 74.3 us -> 69.6 us (0.937)
  Pallas kernels: 71.5 us -> 67.4 us
    pallas_call x3, Pallas kernels: 69.8 us -> 65.7 us  [call(): pl.pallas_call(body, out_shape=tuple((jax.ShapeDtypeStruct(s, d) for s, d...]
where the time goes in v3:
time: 69.6 us; the launch traced here: 69.9 us
  Pallas kernels  67.4 us (97%)
  between operations  1.67 us (2%)
  local copies, waits for them, and re-layouts  0.78 us (1%)
    pallas_call x3, Pallas kernels, call(): pl.pallas_call(body, out_shape=tuple((jax.ShapeDtypeStruct(s, d) for s, d...  65.7 us
    pallas_call x1, Pallas kernels, store(): pl.pallas_call(functools.partial(put_out, count), out_shape=tuple((jax.Sh...  1.73 us

profile of v3, /device:TPU:0, one launch (start us, length us, event | category | flops | bytes accessed | tf_op | source)
XLA Modules:
  0.0 69.9 jit_solution(4702739030881109433)
XLA Ops:
  1.3 0.0 copy-start.13
  1.3 0.0 copy-start.14
  1.3 14.1 %shard_map.189 = (s32[32,1,128]{2,1,0:T(1,128)}, bf16[32,8,256]{2,1,0:T(8,128)(2,1)}) custom-call(bf16[2048,256]{1,0:T(8,128)(2,1)} %feat.1, s32[8,32]{1,0:T(8,128)} %bitcast.19, s32[16,32]{1,0:T(8,128)} %bitcast.25), custom_call_target="tpu_custom_call" | custom-call | flops 10000000000 | bytes 1024 | tf_op jit(solution)/shard_map/pallas_call | solution.py:113
  15.4 0.0 copy-done.13
  15.4 0.0 copy-done.14
  15.4 0.0 copy-start.6
  15.4 0.7 %copy-done.6 = s32[32,1,128]{2,1,0:T(1,128)S(1)} copy-done((s32[32,1,128]{2,1,0:T(1,128)S(1)}, s32[32,1,128]{2,1,0:T(1,128)}, u32[]{:S(2)}) %copy-start.6) | copy-done | bytes 16408
  16.1 0.0 copy-start
  16.1 0.0 copy-start.2
  16.1 0.0 copy-start.4
  16.1 0.0 copy-start.5
  16.1 0.0 copy-start.7
  16.2 0.0 copy-start.8
  16.2 0.0 copy-start.9
  16.2 0.0 copy-start.10
  16.2 0.0 copy-start.11
  16.2 0.0 copy-start.12
  16.2 8.5 %shard_map.190 = (bf16[512,2304]{1,0:T(8,128)(2,1)S(1)}, s32[8,128]{1,0:T(8,128)S(1)}) custom-call(s32[128,128]{1,0:T(8,128)S(1)} %bitcast.23, s32[128,128]{1,0:T(8,128)S(1)} %bitcast.24, s32[1]{0:T(128)S(6)} %copy.21.count_far, s32[32,1,128]{2,1,0:T(1,128)S(1)} %copy-done.6), custom_call_target="tpu_custom_call" | custom-call | flops 10000000000 | bytes 1024 | tf_op jit(solution)/shard_map/pallas_call | solution.py:113
  24.8 0.0 copy-done
  24.8 0.0 copy-done.1
  24.8 0.0 copy-done.2
  24.8 0.0 copy-done.3
  24.8 0.0 copy-done.4
  24.8 0.0 copy-done.5
  24.8 0.0 copy-done.7
  24.8 0.0 copy-done.8
  24.9 0.0 copy-done.9
  24.9 0.0 copy-done.10
  24.9 0.0 copy-done.11
  24.9 0.0 copy-done.12
  24.9 43.1 %shard_map.191 = (f32[1,2048]{1,0:T(1,128)S(1)}, f32[2048,256]{1,0:T(8,128)S(1)}, f32[256,256]{1,0:T(8,128)S(1)}, f32[256,256]{1,0:T(8,128)S(1)}, f32[512,256]{1...) custom-call(bf16[2048,256]{1,0:T(8,128)(2,1)S(1)} %copy-done, bf16[32,8,256]{2,1,0:T(8,128)(2,1)S(1)} %copy-done.4, ...), custom_call_target="tpu_custom_call" | custom-call | tf_op jit(solution)/shard_map/pallas_call | solution.py:113
  68.0 1.7 %shard_map.192 = (f32[1,2048]{1,0:T(1,128)}, f32[2048,256]{1,0:T(8,128)}, f32[256,256]{1,0:T(8,128)}, f32[256,256]{1,0:T(8,128)}, f32[512,256]{1,0:T(8,128)}, /*index=5*/f32[1,256]{1,0:T(1,128)}, f32[1,256]{1,0:T(1,128)}) custom-call(f32[1,2048]{1,0:T(1,128)S(1)} %get-tuple-element.29.refs_0_, f32[2048,256]{1,0:T(8,128)S(1)} %get-tuple-element.30.refs_1_, ...), custom_call_target="tpu_custom_call" | custom-call | tf_op jit(solution)/shard_map/pallas_call | solution.py:482
  (2 shorter events, 0.0 us)
Async XLA Ops:
  1.3 14.1 %copy-start.13 = (s32[16384]{0:T(1024)S(1)}, s32[16384]{0:T(1024)}, u32[]{:S(2)}) copy-start(s32[16384]{0:T(1024)} %param.15) | copy-start | bytes 196612
  1.3 14.1 %copy-start.14 = (s32[16384]{0:T(1024)S(1)}, s32[16384]{0:T(1024)}, u32[]{:S(2)}) copy-start(s32[16384]{0:T(1024)} %param.16) | copy-start | bytes 196612
  15.4 0.7 %copy-start.6 = (s32[32,1,128]{2,1,0:T(1,128)S(1)}, s32[32,1,128]{2,1,0:T(1,128)}, u32[]{:S(2)}) copy-start(s32[32,1,128]{2,1,0:T(1,128)} %get-tuple-element.26.wanted) | copy-start | bytes 49156
  16.1 8.7 %copy-start = (bf16[2048,256]{1,0:T(8,128)(2,1)S(1)}, bf16[2048,256]{1,0:T(8,128)(2,1)}, u32[]{:S(2)}) copy-start(bf16[2048,256]{1,0:T(8,128)(2,1)} %feat.1) | copy-start | bytes 3145732
  16.1 8.7 %copy-start.1 = (bf16[512,256]{1,0:T(8,128)(2,1)S(1)}, bf16[512,256]{1,0:T(8,128)(2,1)}, u32[]{:S(2)}) copy-start(bf16[512,256]{1,0:T(8,128)(2,1)} %w_hidden.1) | copy-start | bytes 786436
  16.1 8.7 %copy-start.2 = (bf16[256,256]{1,0:T(8,128)(2,1)S(1)}, bf16[256,256]{1,0:T(8,128)(2,1)}, u32[]{:S(2)}) copy-start(bf16[256,256]{1,0:T(8,128)(2,1)} %w_self.1) | copy-start | bytes 393220
  16.1 8.7 %copy-start.3 = (bf16[256,256]{1,0:T(8,128)(2,1)S(1)}, bf16[256,256]{1,0:T(8,128)(2,1)}, u32[]{:S(2)}) copy-start(bf16[256,256]{1,0:T(8,128)(2,1)} %w_neigh.1) | copy-start | bytes 393220
  16.1 8.7 %copy-start.4 = (bf16[32,8,256]{2,1,0:T(8,128)(2,1)S(1)}, bf16[32,8,256]{2,1,0:T(8,128)(2,1)}, u32[]{:S(2)}) copy-start(bf16[32,8,256]{2,1,0:T(8,128)(2,1)} %get-tuple-element.25.arrived) | copy-start | bytes 393220
  16.1 8.7 %copy-start.5 = (s32[2048,2]{0,1:T(2,128)S(1)}, s32[2048,2]{0,1:T(2,128)}, u32[]{:S(2)}) copy-start(s32[2048,2]{0,1:T(2,128)} %param.20) | copy-start | bytes 49156
  16.1 8.7 %copy-start.7 = (s32[32,1,128]{2,1,0:T(1,128)S(1)}, s32[32,1,128]{2,1,0:T(1,128)}, u32[]{:S(2)}) copy-start(s32[32,1,128]{2,1,0:T(1,128)} %get-tuple-element.26.wanted) | copy-start | bytes 49156
  16.2 8.7 %copy-start.8 = (s32[2048]{0:T(1024)S(1)}, s32[2048]{0:T(1024)}, u32[]{:S(2)}) copy-start(s32[2048]{0:T(1024)} %param.21) | copy-start | bytes 24580
  16.2 8.7 %copy-start.9 = (f32[2048]{0:T(1024)S(1)}, f32[2048]{0:T(1024)}, u32[]{:S(2)}) copy-start(f32[2048]{0:T(1024)} %param.22) | copy-start | bytes 24580
  16.2 8.7 %copy-start.10 = (s32[1,32,8]{1,2,0:T(8,128)S(1)}, s32[1,32,8]{1,2,0:T(8,128)}, u32[]{:S(2)}) copy-start(s32[1,32,8]{1,2,0:T(8,128)} %param.18) | copy-start | bytes 3076
  16.2 8.7 %copy-start.11 = (f32[256]{0:T(256)S(1)}, f32[256]{0:T(256)}, u32[]{:S(2)}) copy-start(f32[256]{0:T(256)} %param.26) | copy-start | bytes 3076
  16.2 8.7 %copy-start.12 = (f32[256]{0:T(256)S(1)}, f32[256]{0:T(256)}, u32[]{:S(2)}) copy-start(f32[256]{0:T(256)} %param.27) | copy-start | bytes 3076

commit v4 on v3

--- a/solution.py
+++ b/solution.py
@@ -243,13 +243,16 @@
     for b in range(depth // 8):
         @pl.when((b * 8 < longest) | (b * 8 < early * group))
         def _():
-            held = jnp.full((8, 128), -1, jnp.int32)
+            held = [jnp.full((8, 128), -1, jnp.int32) for _ in range(8)]
             for r in range(8 * b, depth):
                 for d in range(merge):
                     to = jnp.broadcast_to(ranks[d, r : r + 1, :], (8, 128))
                     value = jnp.broadcast_to(packs[d, r : r + 1, :], (8, 128))
-                    held = jnp.where(to == steps + 8.0 * b, value, held)
-            dense[8 * b : 8 * b + 8, :] = held
+                    n = (r * merge + d) % len(held)
+                    held[n] = jnp.where(to == steps + 8.0 * b, value, held[n])
+            while len(held) > 1:
+                held = [jnp.maximum(x, y) for x, y in zip(held[::2], held[1::2])]
+            dense[8 * b : 8 * b + 8, :] = held[0]
     head[...] = dense[: head.shape[0], :]
 
     @pl.loop(early, (longest + group - 1) // group)
@@ -271,7 +274,7 @@
     small, small_in, small_part, small_parts,
     grad, self_sent, self_in, self_part, self_parts, self_own, self_all,
     neigh_sent, neigh_in, neigh_part, neigh_parts, neigh_own, neigh_all,
-    near, far, returned, halo_back, feat_t, agg_t,
+    near, far, returned, halo_back, feat_t, agg_t, hidden_t,
     s0, r0, s1, r1, s2, r2, *more,
 ):
     plane, line = Line("dom", dom), Line("grp", grp)
@@ -287,11 +290,14 @@
     counts = counted
     if early:
         counts, edge_marks = extra
-        values = [head[k : k + 1, :] for k in range(head.shape[0])]
-        count_block = mark_edges(values, index, edge_marks, nodes, block)
-        for b in range(table_rows // block):
-            cols = slice(b * block, b * block + block)
-            counts[:, cols] = (counted[:, cols].astype(F32) + count_block(b)).astype(BF16)
+        group = head.shape[0] // early
+        for c in range(early):
+            have = counts if c else counted
+            values = [head[k : k + 1, :] for k in range(c * group, c * group + group)]
+            count_block = mark_edges(values, index, edge_marks, nodes, block)
+            for b in range(table_rows // block):
+                cols = slice(b * block, b * block + block)
+                counts[:, cols] = (have[:, cols].astype(F32) + count_block(b)).astype(BF16)
     for i in range(parts):
         span = slice(i * size, i * size + size)
         degree = jnp.sum(counts[span, :].astype(F32), axis=1, keepdims=True)
@@ -319,13 +325,15 @@
         picks[:rows, span] = equal_mask(slots, end[:1, :])
         picks[rows:, span] = equal_mask(slots, end[1:, :])
 
+    hidden_t[0] = w_hidden[:width, :].T
+    hidden_t[1] = w_hidden[width:, :].T
     bias_col = column_of(bias[...])
     out_col = column_of(w_out[...])
     links.finish(serve)
 
     got = received[...].reshape(rows, width)
-    for place, half in ((0, w_hidden[:width, :]), (rows, w_hidden[width:, :])):
-        exact = dot(got, half).T
+    for i, place in enumerate((0, rows)):
+        exact = dot(hidden_t[i], got, NT)
         upper = exact.astype(BF16)
         upper_lower[:width, place : place + rows] = upper
         upper_lower[width:, place : place + rows] = (exact - upper.astype(F32)).astype(BF16)
@@ -534,10 +542,10 @@
     group = 8
     depth = slots // 128
     merge = 2
-    early = 1 if rows <= 1024 else 0
+    early = 3 if rows <= 1024 else 0
     counts, head = call(
         functools.partial(count_edges, req_len, nodes, block, group, merge, early),
-        [((rows, table_rows), BF16), ((group, 128), jnp.int32)],
+        [((rows, table_rows), BF16), ((max(early, 1) * group, 128), jnp.int32)],
         (edge_src.reshape(depth, 128), edge_dst.reshape(depth, 128), edge_count, wanted),
         [
             pltpu.VMEM((depth, 128), jnp.int32),
@@ -555,7 +563,7 @@
         micros=10,
         limit=min(VMEM_LIMIT, rows * 40 * 1024),
     )
-    chunk = 512
+    chunk = 256
     rows_of = lambda *shape: pltpu.VMEM(shape, BF16)
     found = call(
         functools.partial(middle, dom, grp, req_len, chunk, block, early),
@@ -612,7 +620,8 @@
             rows_of(peers, halo_len, width),
             rows_of(width, rows),
             rows_of(width, rows),
-        ] + sems(peers, 3) + sems(dom, 4) + sems(grp, 5) + sems(dom, 3) + early * [rows_of(rows, table_rows), pltpu.VMEM((rows, group * 128), F8)],
+            rows_of(2, width, width),
+        ] + sems(peers, 3) + sems(dom, 4) + sems(grp, 5) + sems(dom, 3) + min(early, 1) * [rows_of(rows, table_rows), pltpu.VMEM((rows, group * 128), F8)],
         collective_id=1,
         limit=min(VMEM_LIMIT, rows * 60 * 1024),
     )

time: 69.6 us -> 68.4 us (0.983)
  Pallas kernels: 67.4 us -> 65.9 us
    pallas_call x3, Pallas kernels: 65.7 us -> 64.2 us  [call(): pl.pallas_call(body, out_shape=tuple((jax.ShapeDtypeStruct(s, d) for s, d...]
where the time goes in v4:
time: 68.4 us
  Pallas kernels  65.9 us (96%)
  between operations  1.67 us (2%)
  local copies, waits for them, and re-layouts  0.78 us (1%)
    pallas_call x3, Pallas kernels, call(): pl.pallas_call(body, out_shape=tuple((jax.ShapeDtypeStruct(s, d) for s, d...  64.2 us
    pallas_call x1, Pallas kernels, store(): pl.pallas_call(functools.partial(put_out, count), out_shape=tuple((jax.Sh...  1.73 us

profile of v4, /device:TPU:0, one launch (start us, length us, event | category | flops | bytes accessed | tf_op | source)
XLA Modules:
  0.0 68.4 jit_solution(10363109696478749991)
XLA Ops:
  1.3 0.0 copy-start.13
  1.3 0.0 copy-start.14
  1.3 14.1 %shard_map.189 = (s32[32,1,128]{2,1,0:T(1,128)}, bf16[32,8,256]{2,1,0:T(8,128)(2,1)}) custom-call(bf16[2048,256]{1,0:T(8,128)(2,1)} %feat.1, s32[8,32]{1,0:T(8,128)} %bitcast.19, s32[16,32]{1,0:T(8,128)} %bitcast.25), custom_call_target="tpu_custom_call" | custom-call | flops 10000000000 | bytes 1024 | tf_op jit(solution)/shard_map/pallas_call | solution.py:113
  15.4 0.0 copy-done.13
  15.4 0.0 copy-done.14
  15.4 0.0 copy-start.6
  15.4 0.7 %copy-done.6 = s32[32,1,128]{2,1,0:T(1,128)S(1)} copy-done((s32[32,1,128]{2,1,0:T(1,128)S(1)}, s32[32,1,128]{2,1,0:T(1,128)}, u32[]{:S(2)}) %copy-start.6) | copy-done | bytes 16408
  16.1 0.0 copy-start
  16.1 0.0 copy-start.1
  16.1 0.0 copy-start.4
  16.1 0.0 copy-start.5
  16.1 0.0 copy-start.7
  16.2 0.0 copy-start.8
  16.2 0.0 copy-start.9
  16.2 0.0 copy-start.10
  16.2 0.0 copy-start.11
  16.2 0.0 copy-start.12
  16.2 5.2 %shard_map.190 = (bf16[512,2304]{1,0:T(8,128)(2,1)S(1)}, s32[24,128]{1,0:T(8,128)S(1)}) custom-call(s32[128,128]{1,0:T(8,128)S(1)} %bitcast.23, s32[128,128]{1,0:T(8,128)S(1)} %bitcast.24, s32[1]{0:T(128)S(6)} %copy.21.count_far, s32[32,1,128]{2,1,0:T(1,128)S(1)} %copy-done.6), custom_call_target="tpu_custom_call" | custom-call | flops 10000000000 | bytes 1024 | tf_op jit(solution)/shard_map/pallas_call | solution.py:113
  21.4 0.0 copy-done
  21.4 0.0 copy-done.1
  21.4 0.0 copy-done.2
  21.4 0.0 copy-done.3
  21.5 0.0 copy-done.4
  21.5 0.0 copy-done.5
  21.5 0.0 copy-done.7
  21.5 0.0 copy-done.8
  21.5 0.0 copy-done.9
  21.5 0.0 copy-done.10
  21.5 0.0 copy-done.11
  21.5 0.0 copy-done.12
  21.5 45.0 %shard_map.191 = (f32[1,2048]{1,0:T(1,128)S(1)}, f32[2048,256]{1,0:T(8,128)S(1)}, f32[256,256]{1,0:T(8,128)S(1)}, f32[256,256]{1,0:T(8,128)S(1)}, f32[512,256]{1...) custom-call(bf16[2048,256]{1,0:T(8,128)(2,1)S(1)} %copy-done, bf16[32,8,256]{2,1,0:T(8,128)(2,1)S(1)} %copy-done.4, ...), custom_call_target="tpu_custom_call" | custom-call | tf_op jit(solution)/shard_map/pallas_call | solution.py:113
  66.5 1.7 %shard_map.192 = (f32[1,2048]{1,0:T(1,128)}, f32[2048,256]{1,0:T(8,128)}, f32[256,256]{1,0:T(8,128)}, f32[256,256]{1,0:T(8,128)}, f32[512,256]{1,0:T(8,128)}, /*index=5*/f32[1,256]{1,0:T(1,128)}, f32[1,256]{1,0:T(1,128)}) custom-call(f32[1,2048]{1,0:T(1,128)S(1)} %get-tuple-element.29.refs_0_, f32[2048,256]{1,0:T(8,128)S(1)} %get-tuple-element.30.refs_1_, ...), custom_call_target="tpu_custom_call" | custom-call | tf_op jit(solution)/shard_map/pallas_call | solution.py:490
  (2 shorter events, 0.0 us)
Async XLA Ops:
  1.3 14.1 %copy-start.13 = (s32[16384]{0:T(1024)S(1)}, s32[16384]{0:T(1024)}, u32[]{:S(2)}) copy-start(s32[16384]{0:T(1024)} %param.15) | copy-start | bytes 196612
  1.3 14.1 %copy-start.14 = (s32[16384]{0:T(1024)S(1)}, s32[16384]{0:T(1024)}, u32[]{:S(2)}) copy-start(s32[16384]{0:T(1024)} %param.16) | copy-start | bytes 196612
  15.4 0.7 %copy-start.6 = (s32[32,1,128]{2,1,0:T(1,128)S(1)}, s32[32,1,128]{2,1,0:T(1,128)}, u32[]{:S(2)}) copy-start(s32[32,1,128]{2,1,0:T(1,128)} %get-tuple-element.26.wanted) | copy-start | bytes 49156
  16.1 5.3 %copy-start = (bf16[2048,256]{1,0:T(8,128)(2,1)S(1)}, bf16[2048,256]{1,0:T(8,128)(2,1)}, u32[]{:S(2)}) copy-start(bf16[2048,256]{1,0:T(8,128)(2,1)} %feat.1) | copy-start | bytes 3145732
  16.1 5.3 %copy-start.1 = (bf16[512,256]{1,0:T(8,128)(2,1)S(1)}, bf16[512,256]{1,0:T(8,128)(2,1)}, u32[]{:S(2)}) copy-start(bf16[512,256]{1,0:T(8,128)(2,1)} %w_hidden.1) | copy-start | bytes 786436
  16.1 5.3 %copy-start.2 = (bf16[256,256]{1,0:T(8,128)(2,1)S(1)}, bf16[256,256]{1,0:T(8,128)(2,1)}, u32[]{:S(2)}) copy-start(bf16[256,256]{1,0:T(8,128)(2,1)} %w_self.1) | copy-start | bytes 393220
  16.1 5.3 %copy-start.3 = (bf16[256,256]{1,0:T(8,128)(2,1)S(1)}, bf16[256,256]{1,0:T(8,128)(2,1)}, u32[]{:S(2)}) copy-start(bf16[256,256]{1,0:T(8,128)(2,1)} %w_neigh.1) | copy-start | bytes 393220
  16.1 5.3 %copy-start.4 = (bf16[32,8,256]{2,1,0:T(8,128)(2,1)S(1)}, bf16[32,8,256]{2,1,0:T(8,128)(2,1)}, u32[]{:S(2)}) copy-start(bf16[32,8,256]{2,1,0:T(8,128)(2,1)} %get-tuple-element.25.arrived) | copy-start | bytes 393220
  16.1 5.3 %copy-start.5 = (s32[2048,2]{0,1:T(2,128)S(1)}, s32[2048,2]{0,1:T(2,128)}, u32[]{:S(2)}) copy-start(s32[2048,2]{0,1:T(2,128)} %param.20) | copy-start | bytes 49156
  16.1 5.3 %copy-start.7 = (s32[32,1,128]{2,1,0:T(1,128)S(1)}, s32[32,1,128]{2,1,0:T(1,128)}, u32[]{:S(2)}) copy-start(s32[32,1,128]{2,1,0:T(1,128)} %get-tuple-element.26.wanted) | copy-start | bytes 49156
  16.2 5.3 %copy-start.8 = (s32[2048]{0:T(1024)S(1)}, s32[2048]{0:T(1024)}, u32[]{:S(2)}) copy-start(s32[2048]{0:T(1024)} %param.21) | copy-start | bytes 24580
  16.2 5.3 %copy-start.9 = (f32[2048]{0:T(1024)S(1)}, f32[2048]{0:T(1024)}, u32[]{:S(2)}) copy-start(f32[2048]{0:T(1024)} %param.22) | copy-start | bytes 24580
  16.2 5.3 %copy-start.10 = (s32[1,32,8]{1,2,0:T(8,128)S(1)}, s32[1,32,8]{1,2,0:T(8,128)}, u32[]{:S(2)}) copy-start(s32[1,32,8]{1,2,0:T(8,128)} %param.18) | copy-start | bytes 3076
  16.2 5.3 %copy-start.11 = (f32[256]{0:T(256)S(1)}, f32[256]{0:T(256)}, u32[]{:S(2)}) copy-start(f32[256]{0:T(256)} %param.26) | copy-start | bytes 3076
  16.2 5.3 %copy-start.12 = (f32[256]{0:T(256)S(1)}, f32[256]{0:T(256)}, u32[]{:S(2)}) copy-start(f32[256]{0:T(256)} %param.27) | copy-start | bytes 3076

commit v5 on v4

--- a/solution.py
+++ b/solution.py
@@ -53,7 +53,7 @@
             body(self.other(i))
             return carry
 
-        lax.fori_loop(1, self.peers, step, 0)
+        lax.fori_loop(1, self.peers, step, 0, unroll=self.peers - 1 if self.peers <= 32 else 1)
 
     def greet(self):
         barrier = pltpu.get_barrier_semaphore()

time: 68.4 us -> 67.3 us (0.984)
  Pallas kernels: 65.9 us -> 64.8 us
    pallas_call x3, Pallas kernels: 64.2 us -> 63.1 us  [call(): pl.pallas_call(body, out_shape=tuple((jax.ShapeDtypeStruct(s, d) for s, d...]
where the time goes in v5:
time: 67.3 us
  Pallas kernels  64.8 us (96%)
  between operations  1.67 us (2%)
  local copies, waits for them, and re-layouts  0.78 us (1%)
    pallas_call x3, Pallas kernels, call(): pl.pallas_call(body, out_shape=tuple((jax.ShapeDtypeStruct(s, d) for s, d...  63.1 us
    pallas_call x1, Pallas kernels, store(): pl.pallas_call(functools.partial(put_out, count), out_shape=tuple((jax.Sh...  1.73 us

profile of v5, /device:TPU:0, one launch (start us, length us, event | category | flops | bytes accessed | tf_op | source)
XLA Modules:
  0.0 67.3 jit_solution(17699637514553836367)
XLA Ops:
  1.3 0.0 copy-start.13
  1.3 0.0 copy-start.14
  1.3 13.9 %shard_map.189 = (s32[32,1,128]{2,1,0:T(1,128)}, bf16[32,8,256]{2,1,0:T(8,128)(2,1)}) custom-call(bf16[2048,256]{1,0:T(8,128)(2,1)} %feat.1, s32[8,32]{1,0:T(8,128)} %bitcast.19, s32[16,32]{1,0:T(8,128)} %bitcast.25), custom_call_target="tpu_custom_call" | custom-call | flops 10000000000 | bytes 1024 | tf_op jit(solution)/shard_map/pallas_call | solution.py:113
  15.2 0.0 copy-done.13
  15.2 0.0 copy-done.14
  15.2 0.0 copy-start.6
  15.2 0.7 %copy-done.6 = s32[32,1,128]{2,1,0:T(1,128)S(1)} copy-done((s32[32,1,128]{2,1,0:T(1,128)S(1)}, s32[32,1,128]{2,1,0:T(1,128)}, u32[]{:S(2)}) %copy-start.6) | copy-done | bytes 16408
  15.9 0.0 copy-start
  15.9 0.0 copy-start.2
  15.9 0.0 copy-start.4
  15.9 0.0 copy-start.5
  15.9 0.0 copy-start.7
  15.9 0.0 copy-start.8
  16.0 0.0 copy-start.9
  16.0 0.0 copy-start.10
  16.0 0.0 copy-start.11
  16.0 0.0 copy-start.12
  16.0 2.0 %shard_map.190 = (bf16[512,2304]{1,0:T(8,128)(2,1)S(1)}, s32[24,128]{1,0:T(8,128)S(1)}) custom-call(s32[128,128]{1,0:T(8,128)S(1)} %bitcast.23, s32[128,128]{1,0:T(8,128)S(1)} %bitcast.24, s32[1]{0:T(128)S(6)} %copy.21.count_far, s32[32,1,128]{2,1,0:T(1,128)S(1)} %copy-done.6), custom_call_target="tpu_custom_call" | custom-call | flops 10000000000 | bytes 1024 | tf_op jit(solution)/shard_map/pallas_call | solution.py:113
  18.1 0.0 copy-done
  18.1 0.0 copy-done.1
  18.1 0.0 copy-done.2
  18.1 0.0 copy-done.3
  18.1 0.0 copy-done.4
  18.1 0.0 copy-done.5
  18.1 0.0 copy-done.7
  18.1 0.0 copy-done.8
  18.1 0.0 copy-done.9
  18.1 0.0 copy-done.10
  18.2 0.0 copy-done.11
  18.2 0.0 copy-done.12
  18.2 47.2 %shard_map.191 = (f32[1,2048]{1,0:T(1,128)S(1)}, f32[2048,256]{1,0:T(8,128)S(1)}, f32[256,256]{1,0:T(8,128)S(1)}, f32[256,256]{1,0:T(8,128)S(1)}, f32[512,256]{1...) custom-call(bf16[2048,256]{1,0:T(8,128)(2,1)S(1)} %copy-done, bf16[32,8,256]{2,1,0:T(8,128)(2,1)S(1)} %copy-done.4, ...), custom_call_target="tpu_custom_call" | custom-call | tf_op jit(solution)/shard_map/pallas_call | solution.py:113
  65.4 1.7 %shard_map.192 = (f32[1,2048]{1,0:T(1,128)}, f32[2048,256]{1,0:T(8,128)}, f32[256,256]{1,0:T(8,128)}, f32[256,256]{1,0:T(8,128)}, f32[512,256]{1,0:T(8,128)}, /*index=5*/f32[1,256]{1,0:T(1,128)}, f32[1,256]{1,0:T(1,128)}) custom-call(f32[1,2048]{1,0:T(1,128)S(1)} %get-tuple-element.29.refs_0_, f32[2048,256]{1,0:T(8,128)S(1)} %get-tuple-element.30.refs_1_, ...), custom_call_target="tpu_custom_call" | custom-call | tf_op jit(solution)/shard_map/pallas_call | solution.py:490
  (2 shorter events, 0.0 us)
Async XLA Ops:
  1.3 13.9 %copy-start.13 = (s32[16384]{0:T(1024)S(1)}, s32[16384]{0:T(1024)}, u32[]{:S(2)}) copy-start(s32[16384]{0:T(1024)} %param.15) | copy-start | bytes 196612
  1.3 13.9 %copy-start.14 = (s32[16384]{0:T(1024)S(1)}, s32[16384]{0:T(1024)}, u32[]{:S(2)}) copy-start(s32[16384]{0:T(1024)} %param.16) | copy-start | bytes 196612
  15.2 0.7 %copy-start.6 = (s32[32,1,128]{2,1,0:T(1,128)S(1)}, s32[32,1,128]{2,1,0:T(1,128)}, u32[]{:S(2)}) copy-start(s32[32,1,128]{2,1,0:T(1,128)} %get-tuple-element.26.wanted) | copy-start | bytes 49156
  15.9 2.2 %copy-start = (bf16[2048,256]{1,0:T(8,128)(2,1)S(1)}, bf16[2048,256]{1,0:T(8,128)(2,1)}, u32[]{:S(2)}) copy-start(bf16[2048,256]{1,0:T(8,128)(2,1)} %feat.1) | copy-start | bytes 3145732
  15.9 2.2 %copy-start.1 = (bf16[512,256]{1,0:T(8,128)(2,1)S(1)}, bf16[512,256]{1,0:T(8,128)(2,1)}, u32[]{:S(2)}) copy-start(bf16[512,256]{1,0:T(8,128)(2,1)} %w_hidden.1) | copy-start | bytes 786436
  15.9 2.2 %copy-start.2 = (bf16[256,256]{1,0:T(8,128)(2,1)S(1)}, bf16[256,256]{1,0:T(8,128)(2,1)}, u32[]{:S(2)}) copy-start(bf16[256,256]{1,0:T(8,128)(2,1)} %w_self.1) | copy-start | bytes 393220
  15.9 2.2 %copy-start.3 = (bf16[256,256]{1,0:T(8,128)(2,1)S(1)}, bf16[256,256]{1,0:T(8,128)(2,1)}, u32[]{:S(2)}) copy-start(bf16[256,256]{1,0:T(8,128)(2,1)} %w_neigh.1) | copy-start | bytes 393220
  15.9 2.2 %copy-start.4 = (bf16[32,8,256]{2,1,0:T(8,128)(2,1)S(1)}, bf16[32,8,256]{2,1,0:T(8,128)(2,1)}, u32[]{:S(2)}) copy-start(bf16[32,8,256]{2,1,0:T(8,128)(2,1)} %get-tuple-element.25.arrived) | copy-start | bytes 393220
  15.9 2.2 %copy-start.5 = (s32[2048,2]{0,1:T(2,128)S(1)}, s32[2048,2]{0,1:T(2,128)}, u32[]{:S(2)}) copy-start(s32[2048,2]{0,1:T(2,128)} %param.20) | copy-start | bytes 49156
  15.9 2.2 %copy-start.7 = (s32[32,1,128]{2,1,0:T(1,128)S(1)}, s32[32,1,128]{2,1,0:T(1,128)}, u32[]{:S(2)}) copy-start(s32[32,1,128]{2,1,0:T(1,128)} %get-tuple-element.26.wanted) | copy-start | bytes 49156
  15.9 2.2 %copy-start.8 = (s32[2048]{0:T(1024)S(1)}, s32[2048]{0:T(1024)}, u32[]{:S(2)}) copy-start(s32[2048]{0:T(1024)} %param.21) | copy-start | bytes 24580
  16.0 2.2 %copy-start.9 = (f32[2048]{0:T(1024)S(1)}, f32[2048]{0:T(1024)}, u32[]{:S(2)}) copy-start(f32[2048]{0:T(1024)} %param.22) | copy-start | bytes 24580
  16.0 2.2 %copy-start.10 = (s32[1,32,8]{1,2,0:T(8,128)S(1)}, s32[1,32,8]{1,2,0:T(8,128)}, u32[]{:S(2)}) copy-start(s32[1,32,8]{1,2,0:T(8,128)} %param.18) | copy-start | bytes 3076
  16.0 2.2 %copy-start.11 = (f32[256]{0:T(256)S(1)}, f32[256]{0:T(256)}, u32[]{:S(2)}) copy-start(f32[256]{0:T(256)} %param.26) | copy-start | bytes 3076
  16.0 2.2 %copy-start.12 = (f32[256]{0:T(256)S(1)}, f32[256]{0:T(256)}, u32[]{:S(2)}) copy-start(f32[256]{0:T(256)} %param.27) | copy-start | bytes 3076
